TPU v7x, 128 devices: a whole 4x4x4 slice. The times are simulated.
128 devices in a mesh: grp: 16 (over z, x), blk: 8 (over y, core).
Axes of the slice: x: 4, y: 4, z: 4, core: 2. Of those that a mesh axis runs over, the one named last changes fastest.
Arguments:
- embeddings: bfloat16 [65536, 1024], P(('grp', 'blk')), may hold values from -60 to 60
- cluster_ids: int32 [65536], P(('grp', 'blk')), may hold values from 0 to 15, as said below
- rank_key: int32 [65536], P(('grp', 'blk')), may hold values from 0 to 65535, each once
Outputs:
- best: float32 [65536], P(('grp', 'blk'))
Inputs may be any that keep to these rules, and one draw needn't show every extreme that they name: `cluster_ids`: on every device, at most 64 of its rows have cluster ids congruent to one value modulo 16, and for some value exactly that many.
All inputs are finite; a program needn't handle non-finite values.
Results may differ from a plain program's by a relative error of at most 0.0005.
Values may be sent and summed in bfloat16 or wider, within the bound.
A program may use at most 64 MiB of HBM per device.

v0:
```python
import jax
import jax.numpy as jnp
from jax import lax
from jax.sharding import PartitionSpec as P

epsilon = 1e-06


def split_up(x, dim, size):
    before, after = (x.shape[:dim], x.shape[dim + 1 :])
    return jnp.moveaxis(x.reshape(*before, size, -1, *after), dim, 0)


def in_order(parts, dim):
    dims = list(parts.shape[1:])
    dims[dim] *= parts.shape[0]
    return jnp.moveaxis(parts, 0, dim).reshape(dims)


def one_exchange(x, axis, axes, splits, concats):
    sizes = [lax.axis_size(a) for a in axes]
    parts = split_up(x, splits[0], sizes[0])
    parts = jnp.moveaxis(split_up(parts, splits[1] + 1, sizes[1]), 0, 1)
    inside = parts.shape[2:]
    parts = parts.reshape(-1, *inside)
    parts = lax.all_to_all(parts, axis, split_axis=0, concat_axis=0, tiled=True)
    parts = in_order(parts.reshape(*sizes, *inside), concats[0] + 1)
    return in_order(parts, concats[1])


def compare(query, keys):
    unit_q, cluster_q, rank_q = query
    unit_k, cluster_k, rank_k = keys
    score = lax.dot_general(
        unit_q, unit_k, (((1,), (1,)), ((), ())), preferred_element_type=jnp.float32
    )
    same = cluster_q[:, None] == cluster_k[None, :]
    ahead = same & (cluster_k[None, :] >= 0) & (rank_k[None, :] < rank_q[:, None])
    behind = same & (cluster_q[:, None] >= 0) & (rank_q[:, None] < rank_k[None, :])
    return (score, ahead, behind)


def local(embeddings, cluster_ids, rank_key):
    rows = embeddings.shape[0]
    groups = lax.axis_size("grp")
    members = lax.axis_size("blk")
    devices = groups * members
    slot = 2 * rows // devices
    values = embeddings.astype(jnp.float32)
    squares = jnp.sum(values * values, axis=1, keepdims=True)
    unit = (values * lax.rsqrt(squares + epsilon)).astype(jnp.bfloat16)
    owner = cluster_ids % groups
    onehot = (owner[:, None] == jnp.arange(groups, dtype=jnp.int32)[None, :]).astype(jnp.int32)
    running = jnp.sum((jnp.cumsum(onehot, axis=0) - onehot) * onehot, axis=1)
    target = (owner * members + running % members) * slot + running // members
    source = (
        jnp.zeros((devices * slot,), jnp.int32).at[target].set(jnp.arange(rows, dtype=jnp.int32))
    )
    filled = jnp.zeros((devices * slot,), jnp.int32).at[target].set(1) > 0
    send_unit = jnp.where(filled[:, None], unit[source], jnp.zeros((), jnp.bfloat16))
    send_cluster = jnp.where(filled, cluster_ids[source], -1)
    send_rank = rank_key[source]
    moved = (
        one_exchange(
            send_unit.reshape(groups, members, slot, -1),
            ("grp", "blk"),
            ("grp", "blk"),
            (0, 1),
            (0, 1),
        ),
        one_exchange(
            send_cluster.reshape(groups, members, slot),
            ("grp", "blk"),
            ("grp", "blk"),
            (0, 1),
            (0, 1),
        ),
        one_exchange(
            send_rank.reshape(groups, members, slot), ("grp", "blk"), ("grp", "blk"), (0, 1), (0, 1)
        ),
    )
    got_unit = moved[0].reshape(devices * slot, -1)
    got_cluster = moved[1].reshape(devices * slot)
    got_rank = moved[2].reshape(devices * slot)
    mine = (got_unit, got_cluster, got_rank)
    floor = jnp.full((devices * slot,), -1.0, jnp.float32)
    score, ahead, behind = compare(
        mine,
        (
            lax.all_gather(mine[0], "blk", axis=0, tiled=True),
            lax.all_gather(mine[1], "blk", axis=0, tiled=True),
            lax.all_gather(mine[2], "blk", axis=0, tiled=True),
        ),
    )
    found = jnp.maximum(floor, jnp.max(jnp.where(ahead, score, -1.0), axis=1))
    returned = one_exchange(
        found.reshape(groups, members, slot), ("grp", "blk"), ("grp", "blk"), (0, 1), (0, 1)
    ).reshape(devices * slot)
    return returned[target]


def solution(mesh):
    placed = (P(("grp", "blk"), None), P(("grp", "blk")), P(("grp", "blk")))
    return jax.shard_map(
        local, mesh=mesh, in_specs=placed, out_specs=P(("grp", "blk")), check_vma=False
    )
```

profile of v0, /device:TPU:0, one launch (start us, length us, event | category | flops | bytes accessed | tf_op | source)
XLA Modules:
  0.0 204.9 jit_solution(9439609861605158067)
XLA Ops:
  6.5 0.0 copy-start
  6.5 0.0 copy-start.1
  6.5 0.0 all-gather.2.cloned.1.call-start
  6.5 0.8 fusion.19
  7.3 0.7 add_select_fusion.2
  8.0 1.5 fusion
  9.5 1.2 reduce-window.6
  10.7 0.2 slice_reduce_fusion
  10.9 0.1 fusion.4
  11.0 0.7 compare_select_fusion.1
  11.7 2.4 %scatter_custom_fusion.1 = s32[1024]{0:T(1024)S(1)} fusion(s32[512]{0:T(512)S(1)} %compare_select_fusion.1, s32[512]{0:T(512)S(1)} %iota.11, s32[]{:T(128)} %constant.50.clone.1), kind=kCustom, calls=%fused_computation.42 | custom fusion | bytes 4100 | tf_op jit(solution)/shard_map/scatter | solution.py:57
  14.2 2.4 %scatter_custom_fusion = s32[1024]{0:T(1024)S(1)} fusion(s32[512]{0:T(512)S(1)} %compare_select_fusion.1, s32[512]{0:T(512)S(1)} %ne.27, s32[]{:T(128)} %constant.50.clone.1), kind=kCustom, calls=%fused_computation.45 | custom fusion | bytes 4100 | tf_op jit(solution)/shard_map/scatter | solution.py:59
  16.7 0.0 copy-done.1
  16.7 0.0 copy-start.3
  16.7 6.9 %gather_fusion = s32[1024]{0:T(1024)S(1)} fusion(s32[512]{0:T(512)S(1)} %copy-done.1, s32[1024]{0:T(1024)S(1)} %fusion.6), kind=kCustom, calls=%fused_computation | custom fusion | bytes 12288 | tf_op jit(solution)/shard_map/gather | solution.py:61
  23.6 0.1 broadcast_in_dim.46
  23.7 0.0 copy-done.3
  23.7 0.2 fusion.1
  23.9 4.1 %gather_fusion.2 = bf16[1024,1024]{1,0:T(8,128)(2,1)S(1)} fusion(bf16[512,1024]{1,0:T(8,128)(2,1)S(1)} %fusion.1, s32[1024]{0:T(1024)S(1)} %fusion.6), kind=kCustom, calls=%fused_computation.2 | custom fusion | bytes 4198400 | tf_op jit(solution)/shard_map/gather | solution.py:60
  28.0 0.2 bitcast_select_fusion
  28.2 41.4 %all_to_all.20 = bf16[128,1,1,8,1024]{4,3,2,1,0:T(8,128)(2,1)} all-to-all(bf16[128,1,1,8,1024]{4,3,2,1,0:T(8,128)(2,1)S(1)} %bitcast_select_fusion), channel_id=1, replica_groups=mesh['grp'=16,'blk'=8] {'grp','blk'}, dimensions={0} | all-to-all | bytes 4194304 | tf_op jit(solution)/shard_map/all_to_all | solution.py:26
  69.7 0.0 all-gather.2.cloned.1.call-update
  69.7 0.7 reshape_transpose_transpose_reshape_reshape_reshape.8
  70.4 4.5 %all-to-all-start = ((s32[128,1,1,8]{3,2,1,0:T(1,128)}), s32[128,1,1,8]{3,2,1,0:T(1,128)S(1)}, u32[]{:S(2)}, u32[]{:S(2)}) async-start(s32[128,1,1,8]{3,2,1,0:T(1,128)} %bitcast.2), calls=%async_computation | async-start | bytes 131072 | tf_op jit(solution)/shard_map/all_to_all | solution.py:26
  74.9 0.0 copy-done
  74.9 0.0 copy-start.2
  75.0 6.9 %gather_fusion.1 = s32[1024]{0:T(1024)S(1)} fusion(s32[512]{0:T(512)S(1)} %copy-done, s32[1024]{0:T(1024)S(1)} %fusion.6), kind=kCustom, calls=%fused_computation.1 | custom fusion | bytes 12288 | tf_op jit(solution)/shard_map/gather | solution.py:62
  81.8 0.7 reshape_transpose_transpose_reshape_reshape_reshape.9
  82.5 1.7 all-to-all-done
  84.3 8.0 %all-to-all-start.1 = ((s32[128,1,1,8]{3,2,1,0:T(1,128)}), s32[128,1,1,8]{3,2,1,0:T(1,128)S(1)}, u32[]{:S(2)}, u32[]{:S(2)}) async-start(s32[128,1,1,8]{3,2,1,0:T(1,128)} %bitcast.7), calls=%async_computation.1 | async-start | bytes 131072 | tf_op jit(solution)/shard_map/all_to_all | solution.py:26
  92.3 0.1 eq.48
  92.4 9.2 %all-to-all-done.1 = s32[128,1,1,8]{3,2,1,0:T(1,128)S(1)} async-done(((s32[128,1,1,8]{3,2,1,0:T(1,128)}), s32[128,1,1,8]{3,2,1,0:T(1,128)S(1)}, u32[]{:S(2)}, u32[]{:S(2)}) %all-to-all-start.1) | async-done | bytes 4128 | tf_op jit(solution)/shard_map/all_to_all | solution.py:26
  101.6 0.1 reshape_reshape.10
  101.7 13.1 %all_gather.9 = s32[8192]{0:T(1024)S(1)} all-gather(s32[1024]{0:T(1024)S(1)} %eq.48), channel_id=1, replica_groups=mesh['grp'=16,'blk'=8] {'blk'}, dimensions={0}, use_global_device_ids=true | all-gather | bytes 36864 | tf_op jit(solution)/shard_map/all_gather | solution.py:91
  114.9 13.3 %all_gather.10 = s32[8192]{0:T(1024)S(1)} all-gather(s32[1024]{0:T(1024)S(1)} %reshape_reshape.10), channel_id=1, replica_groups=mesh['grp'=16,'blk'=8] {'blk'}, dimensions={0}, use_global_device_ids=true | all-gather | bytes 36864 | tf_op jit(solution)/shard_map/all_gather | solution.py:92
  128.1 22.9 %all-gather.2.cloned.1.call-done = bf16[8192,1024]{1,0:T(8,128)(2,1)} async-done(((bf16[1024,1024]{1,0:T(8,128)(2,1)}), bf16[8192,1024]{1,0:T(8,128)(2,1)}) %all-gather.2.cloned.1.call-update) | async-done | bytes 16777232 | tf_op jit(solution)/shard_map/all_gather | solution.py:90
  151.0 0.0 copy-done.2
  151.0 24.5 %select_reduce_fusion = f32[1024]{0:T(1024)S(1)} fusion(bf16[8192,1024]{1,0:T(8,128)(2,1)} %all-gather.2.cloned.1.call-done, s32[8192]{0:T(1024)S(1)} %all_gather.10, s32[8192]{0:T(1024)S(1)} %all_gather.9, s32[1024]{0:T(1024)S(1)} %reshape_reshape.10, s32[1024]{0:T(1024)S(1)} %eq.48, pred[8192]{0:T(1024)(128)(4,1)S(1)} %broadcast_compare_fusion, ...), kind=kOutput, calls=%fused_computation.6 | convolution fusion | flops 17230200832 | bytes 18960384 | tf_op jit(solution)/shard_map/dot_general | solution.py:34
  175.5 0.7 max_broadcast_in_dim.14
  176.2 9.0 %all-to-all-start.3 = ((f32[128,1,1,8]{3,2,1,0:T(1,128)}), f32[128,1,1,8]{3,2,1,0:T(1,128)S(1)}, u32[]{:S(2)}, u32[]{:S(2)}) async-start(f32[128,1,1,8]{3,2,1,0:T(1,128)} %bitcast.23), calls=%async_computation.3 | async-start | bytes 131072 | tf_op jit(solution)/shard_map/all_to_all | solution.py:26
  185.2 9.3 %all-to-all-done.3 = f32[128,1,1,8]{3,2,1,0:T(1,128)S(1)} async-done(((f32[128,1,1,8]{3,2,1,0:T(1,128)}), f32[128,1,1,8]{3,2,1,0:T(1,128)S(1)}, u32[]{:S(2)}, u32[]{:S(2)}) %all-to-all-start.3) | async-done | bytes 4128 | tf_op jit(solution)/shard_map/all_to_all | solution.py:26
  194.6 0.1 reshape_reshape.12
  194.6 3.4 %gather_fusion.3 = f32[512]{0:T(512)} fusion(f32[1024]{0:T(1024)S(1)} %reshape_reshape.12, s32[1024]{0:T(1024)S(1)} %pad_clamp_fusion), kind=kCustom, calls=%fused_computation.3 | custom fusion | bytes 6144 | tf_op jit(solution)/shard_map/gather | solution.py:99
  (11 shorter events, 0.1 us)
Async XLA Ops:
  6.5 68.4 %copy-start = (s32[512]{0:T(512)S(1)}, s32[512]{0:T(512)}, u32[]{:S(2)}) copy-start(s32[512]{0:T(512)} %param.5) | copy-start | bytes 6148
  6.5 10.1 %copy-start.1 = (s32[512]{0:T(512)S(1)}, s32[512]{0:T(512)}, u32[]{:S(2)}) copy-start(s32[512]{0:T(512)} %param.4) | copy-start | bytes 6148
  6.5 144.5 %all-gather.2.cloned.1.call-start = ((), (), s32[]{:S(2)}) async-start(), calls=%async_computation.4 | async-start | bytes 18874368 | tf_op jit(solution)/shard_map/all_gather | solution.py:90
  16.7 7.0 %copy-start.3 = (bf16[512,1024]{1,0:T(8,128)(2,1)S(1)}, bf16[512,1024]{1,0:T(8,128)(2,1)}, u32[]{:S(2)}) copy-start(bf16[512,1024]{1,0:T(8,128)(2,1)} %param.3) | copy-start | bytes 3145732
  70.4 13.9 %all-to-all-start = ((s32[128,1,1,8]{3,2,1,0:T(1,128)}), s32[128,1,1,8]{3,2,1,0:T(1,128)S(1)}, u32[]{:S(2)}, u32[]{:S(2)}) async-start(s32[128,1,1,8]{3,2,1,0:T(1,128)} %bitcast.2), calls=%async_computation | async-start | bytes 131072 | tf_op jit(solution)/shard_map/all_to_all | solution.py:26
  74.9 76.1 %copy-start.2 = (bf16[128,1,1,8,1024]{4,3,2,1,0:T(8,128)(2,1)S(1)}, bf16[128,1,1,8,1024]{4,3,2,1,0:T(8,128)(2,1)}, u32[]{:S(2)}) copy-start(bf16[128,1,1,8,1024]{4,3,2,1,0:T(8,128)(2,1)} %all_to_all.20) | copy-start | bytes 6291460
  84.3 17.4 %all-to-all-start.1 = ((s32[128,1,1,8]{3,2,1,0:T(1,128)}), s32[128,1,1,8]{3,2,1,0:T(1,128)S(1)}, u32[]{:S(2)}, u32[]{:S(2)}) async-start(s32[128,1,1,8]{3,2,1,0:T(1,128)} %bitcast.7), calls=%async_computation.1 | async-start | bytes 131072 | tf_op jit(solution)/shard_map/all_to_all | solution.py:26
  176.2 18.3 %all-to-all-start.3 = ((f32[128,1,1,8]{3,2,1,0:T(1,128)}), f32[128,1,1,8]{3,2,1,0:T(1,128)S(1)}, u32[]{:S(2)}, u32[]{:S(2)}) async-start(f32[128,1,1,8]{3,2,1,0:T(1,128)} %bitcast.23), calls=%async_computation.3 | async-start | bytes 131072 | tf_op jit(solution)/shard_map/all_to_all | solution.py:26
Sparse Core Ops, SparseCore 0:
  69.8 81.1 all-gather.1
where the time goes:
time: 206 us; the launch traced here: 205 us
  blocking collectives  67.8 us (33%)
  waiting for transfers between devices  43.2 us (21%)
  local copies, waits for them, and re-layouts  28.8 us (14%)
  matrix products  24.5 us (12%)
  starting transfers between devices  21.6 us (10%)
  between operations  13.6 us (7%)
  other arithmetic  5.44 us (3%)
    all_to_all x1, blocking collectives, one_exchange(): parts = lax.all_to_all(parts, axis, split_axis=0, concat_axis=0, tiled=True)  41.4 us
    dot_general x1, matrix products, compare(): lax.dot_general(unit_q, unit_k, (((1,), (1,)), ((), ())), preferred_eleme...  24.5 us
    all_gather x1, waiting for transfers between devices, local(): lax.all_gather(mine[0], 'blk', axis=0, tiled=True)  22.9 us
    all_to_all x3, starting transfers between devices, one_exchange(): parts = lax.all_to_all(parts, axis, split_axis=0, concat_axis=0, tiled=True)  21.6 us
    all_to_all x3, waiting for transfers between devices, one_exchange(): parts = lax.all_to_all(parts, axis, split_axis=0, concat_axis=0, tiled=True)  20.3 us
    all_gather x1, blocking collectives, local(): lax.all_gather(mine[2], 'blk', axis=0, tiled=True)  13.3 us
    all_gather x1, blocking collectives, local(): lax.all_gather(mine[1], 'blk', axis=0, tiled=True)  13.1 us
    gather x1, local copies, waits for them, and re-layouts, local(): send_cluster = jnp.where(filled, cluster_ids[source], -1)  6.87 us
  transfers between devices with their start and end apart: 4, of which 4 were waited for; matrix products, arithmetic and copies ran while one was open for 4% of the time, Pallas kernels for 0%

commit v1 on v0

v1 whole, which is shorter than its diff:
```python
import functools

import jax
import jax.numpy as jnp
from jax import lax
from jax.experimental import pallas as pl
from jax.experimental.pallas import tpu as pltpu
from jax.sharding import PartitionSpec as P

MESH = pl.DeviceIdType.MESH
epsilon = 1e-06
FAR = 1.0e6
OWN, PARTNER, NEXT, CROSS, PREV = range(5)
LAG = 8


def kernel(
    emb_ref, cl_ref, rk_ref, out_ref,
    buf, send, onehot, meta_send, meta_recv, rank_lane, rank_sub, lane_acc, sub_acc,
    part_send, part_recv, final, back_recv,
    meta_s, meta_r, own_s, own_r, rank_s, rank_r, part_s, part_r, back_s, back_r,
    *, groups, members, slot,
):
    rows, depth = emb_ref.shape
    slots = groups * slot
    chips = members // 2
    group, member = lax.axis_index("grp"), lax.axis_index("blk")
    chip, core = member // 2, lax.rem(member, 2)
    after, before = lax.rem(chip + 1, chips), lax.rem(chip + chips - 1, chips)
    partner = {"blk": chip * 2 + 1 - core}
    next_same, next_other = {"blk": after * 2 + core}, {"blk": after * 2 + 1 - core}
    prev_same, prev_other = {"blk": before * 2 + core}, {"blk": before * 2 + 1 - core}

    def ahead(k):
        return {"grp": lax.rem(group + k, groups)}

    def behind(k):
        return {"grp": lax.rem(group + groups - k, groups)}

    barrier = pltpu.get_barrier_semaphore()

    def greet(k, carry):
        pl.semaphore_signal(barrier, inc=1, device_id=ahead(k), device_id_type=MESH)
        return carry

    lax.fori_loop(1, groups, greet, 0)
    for peer in (partner, next_same, next_other, prev_same, prev_other):
        pl.semaphore_signal(barrier, inc=1, device_id=peer, device_id_type=MESH)

    def copy(src, dst, ssem, rsem, peer):
        return pltpu.make_async_remote_copy(
            src_ref=src, dst_ref=dst, send_sem=ssem, recv_sem=rsem,
            device_id=peer, device_id_type=MESH,
        )

    def piece(k):
        return pl.ds(pl.multiple_of(k * slot, slot), slot)

    def exchange(k):
        return copy(send.at[piece(k)], buf.at[OWN, piece(k)], own_s.at[OWN], own_r.at[OWN, k], ahead(k))

    def to_partner(k):
        return copy(buf.at[OWN, piece(k)], buf.at[PARTNER, piece(k)], own_s.at[PARTNER], own_r.at[PARTNER, k], partner)

    def to_prev(k):
        return copy(buf.at[OWN, piece(k)], buf.at[NEXT, piece(k)], own_s.at[NEXT], own_r.at[NEXT, k], prev_same)

    def to_next(k):
        return copy(buf.at[OWN, piece(k)], buf.at[PREV, piece(k)], own_s.at[PREV], own_r.at[PREV, k], next_same)

    def across(k):
        return copy(buf.at[NEXT, piece(k)], buf.at[CROSS, piece(k)], own_s.at[CROSS], own_r.at[CROSS, k], partner)

    def meta(k):
        return copy(meta_send.at[k], meta_recv.at[k], meta_s, meta_r.at[k], ahead(k))

    away = lax.bitwise_and(cl_ref[...] + (groups - group), groups - 1)
    lines = lax.broadcasted_iota(jnp.int32, (groups, rows), 0)
    mine = away == lines
    earlier = lax.broadcasted_iota(jnp.int32, (rows, rows), 0) < lax.broadcasted_iota(jnp.int32, (rows, rows), 1)
    count = jnp.dot(
        jnp.where(mine, 1.0, 0.0).astype(jnp.bfloat16),
        jnp.where(earlier, 1.0, 0.0).astype(jnp.bfloat16),
        preferred_element_type=jnp.float32,
    )
    target = jnp.sum(
        jnp.where(mine, count + (lines * slot).astype(jnp.float32), 0.0), axis=0, keepdims=True
    )
    part = 4 * slot
    for j in range(slots // part):
        at = (lax.broadcasted_iota(jnp.int32, (part, rows), 0) + j * part).astype(jnp.float32)
        onehot[j * part : (j + 1) * part, :] = jnp.where(at == target, 1.0, 0.0).astype(jnp.bfloat16)

    rank = rk_ref[...]
    line8 = lax.broadcasted_iota(jnp.int32, (8, rows), 0)
    high = lax.shift_right_logical(rank, 8).astype(jnp.float32)
    low = lax.bitwise_and(rank, 255).astype(jnp.float32)
    table = jnp.where(line8 == 0, high, jnp.where(line8 == 1, low, 1.0)).astype(jnp.bfloat16)
    found = lax.dot_general(
        table, onehot[...], (((1,), (1,)), ((), ())), preferred_element_type=jnp.float32
    )
    place = found[0:1] * 256.0 + found[1:2] + (1.0 - found[2:3]) * FAR
    left = lax.broadcasted_iota(jnp.int32, (8, 128), 1) < slot
    for t in range(slots // 128):
        tile = jnp.broadcast_to(place[:, t * 128 : (t + 1) * 128], (8, 128))
        turned = pltpu.roll(tile, slot, 1)
        meta_send[2 * t] = jnp.where(left, tile, turned)
        meta_send[2 * t + 1] = jnp.where(left, turned, tile)

    values = emb_ref[...].astype(jnp.float32)
    squares = jnp.sum(values * values, axis=1, keepdims=True)
    unit = (values * lax.rsqrt(squares + epsilon)).astype(jnp.bfloat16)

    for j in range(slots // part):
        packed = jnp.dot(
            onehot[j * part : (j + 1) * part, :], unit, preferred_element_type=jnp.float32
        ).astype(jnp.bfloat16)
        send[j * part : (j + 1) * part, :] = packed
        if j == 0:
            buf[OWN, 0:slot, :] = packed[0:slot]
            pl.semaphore_wait(barrier, groups - 1 + 5)
            for k in range(1, groups):
                meta(k).start()
        for k in range(4 * j, 4 * j + 4):
            if k > 0:
                exchange(k).start()
            else:
                to_prev(0).start()
                to_next(0).start()
                to_partner(0).start()

    lane_acc[...] = jnp.full(lane_acc.shape, -1.0, jnp.float32)
    sub_acc[...] = jnp.full(sub_acc.shape, -1.0, jnp.float32)

    for k in range(1, groups):
        meta(k).wait_recv()
    for t in range(slots // 128):
        first = meta_send[0] if t == 0 else meta_recv[2 * t]
        rank_lane[OWN, t : t + 1, :] = jnp.where(left, first, meta_recv[2 * t + 1])[0:1]
    rank_copies = [
        copy(rank_lane.at[OWN], rank_lane.at[PARTNER], rank_s.at[PARTNER], rank_r.at[PARTNER], partner),
        copy(rank_lane.at[OWN], rank_lane.at[NEXT], rank_s.at[NEXT], rank_r.at[NEXT], prev_same),
        copy(rank_lane.at[OWN], rank_lane.at[PREV], rank_s.at[PREV], rank_r.at[PREV], next_same),
        copy(rank_lane.at[NEXT], rank_lane.at[CROSS], rank_s.at[CROSS], rank_r.at[CROSS], partner),
    ]
    for c in rank_copies[:3]:
        c.start()

    def spread(which):
        for t in range(slots // 128):
            tile = jnp.broadcast_to(rank_lane[which, t : t + 1, :], (128, 128))
            rank_sub[which, t * 128 : (t + 1) * 128, :] = jnp.transpose(tile)

    def relay(k):
        to_prev(k).wait_recv()
        across(k).start()

    def onward(k, carry):
        exchange(k).wait_recv()
        to_prev(k).start()
        to_next(k).start()
        to_partner(k).start()

        @pl.when(k >= LAG)
        def _():
            relay(k - LAG)

        return carry

    half = groups // 2
    lax.fori_loop(1, half, onward, 0)
    spread(OWN)
    rank_copies[0].wait_recv()
    rank_copies[1].wait_recv()
    rank_copies[3].start()
    spread(PARTNER)
    spread(NEXT)
    rank_copies[2].wait_recv()
    rank_copies[3].wait_recv()
    spread(CROSS)
    lax.fori_loop(half, groups, onward, 0)

    def score(x, x0, y, lanes, subs):
        at = pl.ds(x0, part)
        here = rank_sub[x, at, :]
        best = jnp.full((part, 128), -1.0, jnp.float32)
        for n in range(slots // 256):
            s = lax.dot_general(
                buf[x, at, :], buf[y, n * 256 : (n + 1) * 256, :], (((1,), (1,)), ((), ())),
                preferred_element_type=jnp.float32,
            )
            for h in range(2):
                t = 2 * n + h
                sh = s[:, h * 128 : (h + 1) * 128]
                there = rank_lane[y, t : t + 1, :]
                up = jnp.where(here < there, sh, -1.0)
                lane_acc[lanes, t] = jnp.maximum(lane_acc[lanes, t], jnp.max(up.reshape(part // 8, 8, 128), axis=0))
                if subs is not None:
                    best = jnp.maximum(best, jnp.where(there < here, sh, -1.0))
        if subs is not None:
            sub_acc[subs, at, :] = jnp.maximum(sub_acc[subs, at, :], best)

    def square(x, x0, y0):
        here = rank_sub[x, pl.ds(x0, part), :]
        s = lax.dot_general(
            buf[x, pl.ds(x0, part), :], buf[PREV, pl.ds(y0, part), :], (((1,), (1,)), ((), ())),
            preferred_element_type=jnp.float32,
        )
        best = jnp.full((part, 128), -1.0, jnp.float32)
        for h in range(part // 128):
            t = y0 // 128 + h
            sh = s[:, h * 128 : (h + 1) * 128]
            there = rank_lane[PREV, pl.ds(t, 1), :]
            up = jnp.where(here < there, sh, -1.0)
            lane_acc[1, t] = jnp.maximum(lane_acc[1, t], jnp.max(up.reshape(part // 8, 8, 128), axis=0))
            best = jnp.maximum(best, jnp.where(there < here, sh, -1.0))
        at = pl.ds(x0, part)
        sub_acc[x - NEXT, at, :] = jnp.maximum(sub_acc[x - NEXT, at, :], best)

    parts = slots // part
    far = NEXT + chip // (chips // 2)

    def own_rows(i, carry):
        score(OWN, pl.multiple_of(i * part, part), OWN, 0, None)
        return carry

    lax.fori_loop(0, parts, own_rows, 0)

    def take(which):
        def step(k, carry):
            which(k).wait_recv()
            return carry
        return step

    lax.fori_loop(0, groups, take(to_partner), 0)

    def partner_rows(i, carry):
        score(PARTNER, pl.multiple_of(i * part, part), OWN, 0, None)
        return carry

    lax.fori_loop(0, parts, partner_rows, 0)

    def arrived(j, carry):
        @pl.when(j >= LAG // 4)
        def _():
            def step(k, c):
                relay(k)
                return c
            lax.fori_loop(4 * j, 4 * j + 4, step, 0)

        x0 = pl.multiple_of(j * part, part)
        score(NEXT, x0, OWN, 0, 0)
        lax.fori_loop(4 * j, 4 * j + 4, take(across), 0)
        score(CROSS, x0, OWN, 0, 1)
        lax.fori_loop(4 * j, 4 * j + 4, take(to_next), 0)

        def upto(i, c):
            square(far, pl.multiple_of(i * part, part), x0)
            return c

        lax.fori_loop(0, j + 1, upto, 0)

        def below(i, c):
            square(far, x0, pl.multiple_of(i * part, part))
            return c

        lax.fori_loop(0, j, below, 0)
        return carry

    lax.fori_loop(0, parts, arrived, 0)

    for t in range(slots // 128):
        line = slice(t, t + 1)
        for which in range(2):
            tile = jnp.transpose(sub_acc[which, t * 128 : (t + 1) * 128, :])
            part_send[which, line, :] = jnp.max(tile, axis=0, keepdims=True)
        part_send[2, line, :] = jnp.max(lane_acc[1, t], axis=0, keepdims=True)
        final[line, :] = jnp.max(lane_acc[0, t], axis=0, keepdims=True)
    part_copies = [
        copy(part_send.at[i], part_recv.at[i], part_s.at[i], part_r.at[i], peer)
        for i, peer in enumerate((next_same, next_other, prev_same))
    ]
    for c in part_copies:
        c.start()
    for c in part_copies:
        c.wait_recv()
    final[...] = jnp.maximum(
        jnp.maximum(final[...], part_recv[0]), jnp.maximum(part_recv[1], part_recv[2])
    )

    def back(k):
        return copy(final, back_recv.at[k], back_s, back_r.at[k], behind(k))

    for k in range(1, groups):
        back(k).start()
    for k in range(1, groups):
        back(k).wait_recv()
    lines = []
    for t in range(slots // 128):
        line = slice(t, t + 1)
        first = final[line, :] if t == 0 else back_recv[2 * t, line, :]
        lines.append(jnp.where(left[0:1], first, back_recv[2 * t + 1, line, :]))
    got = jnp.concatenate(lines, axis=1)
    one = got.astype(jnp.bfloat16)
    rest = got - one.astype(jnp.float32)
    two = rest.astype(jnp.bfloat16)
    three = rest - two.astype(jnp.float32)
    line8 = lax.broadcasted_iota(jnp.int32, (8, slots), 0)
    terms = jnp.where(
        line8 == 0, one.astype(jnp.float32),
        jnp.where(line8 == 1, two.astype(jnp.float32), jnp.where(line8 == 2, three, 0.0)),
    ).astype(jnp.bfloat16)
    out = jnp.dot(terms, onehot[...], preferred_element_type=jnp.float32)
    out_ref[...] = jnp.sum(out, axis=0, keepdims=True)

    copy(send.at[slot:slots], buf.at[OWN, slot:slots], own_s.at[OWN], own_r.at[OWN, 1], partner).wait_send()
    for which in (PARTNER, NEXT, PREV, CROSS):
        copy(buf.at[OWN], buf.at[which], own_s.at[which], own_r.at[which, 0], partner).wait_send()
    copy(meta_send.at[1:groups], meta_recv.at[1:groups], meta_s, meta_r.at[1], partner).wait_send()
    for c in rank_copies + part_copies:
        c.wait_send()
    copy(meta_send.at[1:groups], back_recv.at[1:groups], back_s, back_r.at[1], partner).wait_send()


def local(embeddings, cluster_ids, rank_key):
    rows, depth = embeddings.shape
    groups, members = lax.axis_size("grp"), lax.axis_size("blk")
    slot = 2 * rows // groups
    slots = groups * slot
    dma = pltpu.SemaphoreType.DMA
    out = pl.pallas_call(
        functools.partial(kernel, groups=groups, members=members, slot=slot),
        out_shape=jax.ShapeDtypeStruct((1, rows), jnp.float32),
        in_specs=[pl.BlockSpec(memory_space=pltpu.VMEM)] * 3,
        out_specs=pl.BlockSpec(memory_space=pltpu.VMEM),
        scratch_shapes=[
            pltpu.VMEM((5, slots, depth), jnp.bfloat16),
            pltpu.VMEM((slots, depth), jnp.bfloat16),
            pltpu.VMEM((slots, rows), jnp.bfloat16),
            pltpu.VMEM((groups, 8, 128), jnp.float32),
            pltpu.VMEM((groups, 8, 128), jnp.float32),
            pltpu.VMEM((5, slots // 128, 128), jnp.float32),
            pltpu.VMEM((4, slots, 128), jnp.float32),
            pltpu.VMEM((2, slots // 128, 8, 128), jnp.float32),
            pltpu.VMEM((2, slots, 128), jnp.float32),
            pltpu.VMEM((3, slots // 128, 128), jnp.float32),
            pltpu.VMEM((3, slots // 128, 128), jnp.float32),
            pltpu.VMEM((slots // 128, 128), jnp.float32),
            pltpu.VMEM((groups, slots // 128, 128), jnp.float32),
            dma, dma((groups,)),
            dma((5,)), dma((5, groups)),
            dma((5,)), dma((5,)),
            dma((3,)), dma((3,)),
            dma, dma((groups,)),
        ],
        compiler_params=pltpu.CompilerParams(
            collective_id=0, has_side_effects=True, vmem_limit_bytes=48 * 1024 * 1024
        ),
    )(embeddings, cluster_ids.reshape(1, rows), rank_key.reshape(1, rows))
    return out.reshape(rows)


def solution(mesh):
    placed = (P(("grp", "blk"), None), P(("grp", "blk")), P(("grp", "blk")))
    return jax.shard_map(
        local, mesh=mesh, in_specs=placed, out_specs=P(("grp", "blk")), check_vma=False
    )
```

time: 206 us -> 84.1 us (0.41)
  Pallas kernels: 0 us -> 80.6 us
  blocking collectives: 67.8 us -> 0 us
  waiting for transfers between devices: 43.2 us -> 0 us
  local copies, waits for them, and re-layouts: 28.8 us -> 3.17 us
  matrix products: 24.5 us -> 0 us
  starting transfers between devices: 21.6 us -> 0 us
  between operations: 13.6 us -> 0.01 us
  other arithmetic: 5.44 us -> 0 us
    pallas_call x0 -> x1, Pallas kernels: none -> 80.6 us  [local(): pl.pallas_call(functools.partial(kernel, groups=groups, members=members,...]
    all_to_all x1 -> x0, blocking collectives: 41.4 us -> none  [one_exchange(): parts = lax.all_to_all(parts, axis, split_axis=0, concat_axis=0, tiled=True)]
    all_gather x2 -> x0, blocking collectives: 26.4 us -> none  [the longest x1 13.3 us: local(): lax.all_gather(mine[2], 'blk', axis=0, tiled=True)]
    dot_general x1 -> x0, matrix products: 24.5 us -> none  [compare(): lax.dot_general(unit_q, unit_k, (((1,), (1,)), ((), ())), preferred_eleme...]
    all_gather x1 -> x0, waiting for transfers between devices: 22.9 us -> none  [local(): lax.all_gather(mine[0], 'blk', axis=0, tiled=True)]
    all_to_all x3 -> x0, starting transfers between devices: 21.6 us -> none  [one_exchange(): parts = lax.all_to_all(parts, axis, split_axis=0, concat_axis=0, tiled=True)]
    gather x4 -> x0, local copies, waits for them, and re-layouts: 21.2 us -> none  [the longest x1 6.87 us: local(): send_cluster = jnp.where(filled, cluster_ids[source], -1)]
    all_to_all x3 -> x0, waiting for transfers between devices: 20.3 us -> none  [one_exchange(): parts = lax.all_to_all(parts, axis, split_axis=0, concat_axis=0, tiled=True)]
  transfers between devices with their start and end apart: 4 -> 0, of which waited for: 4 -> 0; matrix products, arithmetic and copies ran while one was open for 4% -> 0% of each run, Pallas kernels for 0% -> 0%
where the time goes in v1:
time: 84.1 us; the launch traced here: 83.8 us
  Pallas kernels  80.6 us (96%)
  local copies, waits for them, and re-layouts  3.17 us (4%)
    pallas_call x1, Pallas kernels, local(): pl.pallas_call(functools.partial(kernel, groups=groups, members=members,...  80.6 us
    unnamed x7, local copies, waits for them, and re-layouts  3.17 us

profile of v1, /device:TPU:0, one launch (start us, length us, event | category | flops | bytes accessed | tf_op | source)
XLA Modules:
  0.0 83.8 jit_solution(2357124079424790420)
XLA Ops:
  0.0 0.0 copy-start.1
  0.0 0.7 copy-done.1
  0.7 0.0 copy-start
  0.7 1.2 %copy-done = bf16[512,1024]{1,0:T(8,128)(2,1)S(1)} copy-done((bf16[512,1024]{1,0:T(8,128)(2,1)S(1)}, bf16[512,1024]{1,0:T(8,128)(2,1)}, u32[]{:S(2)}) %copy-start) | copy-done | bytes 1048600
  1.9 0.0 copy-start.2
  1.9 0.7 copy-done.2
  2.6 80.6 %shard_map.37 = f32[1,512]{1,0:T(1,128)S(1)} custom-call(bf16[512,1024]{1,0:T(8,128)(2,1)S(1)} %copy-done, s32[1,512]{1,0:T(1,128)S(1)} %bitcast.4, s32[1,512]{1,0:T(1,128)S(1)} %bitcast.5), custom_call_target="tpu_custom_call" | custom-call | tf_op jit(solution)/shard_map/pallas_call | solution.py:331
  83.2 0.6 copy.5
Async XLA Ops:
  0.0 0.7 copy-start.1
  0.7 1.2 %copy-start = (bf16[512,1024]{1,0:T(8,128)(2,1)S(1)}, bf16[512,1024]{1,0:T(8,128)(2,1)}, u32[]{:S(2)}) copy-start(bf16[512,1024]{1,0:T(8,128)(2,1)} %emb_ref.1) | copy-start | bytes 3145732
  1.9 0.7 copy-start.2

commit v2 on v1

v2 whole, which is shorter than its diff:
```python
import functools

import jax
import jax.numpy as jnp
from jax import lax
from jax.experimental import pallas as pl
from jax.experimental.pallas import tpu as pltpu
from jax.sharding import PartitionSpec as P

MESH = pl.DeviceIdType.MESH
epsilon = 1e-06
FAR = 1.0e6
OWN, PARTNER, NEXT, CROSS, PREV = range(5)
LAG = 6


STEPS = (
    (0, 0), (0, 1), (0, 3), (1, 0), (3, 0), (1, 1), (3, 3), (1, 3),
    (3, 1), (0, 2), (2, 0), (1, 2), (2, 1), (3, 2), (2, 3), (2, 2),
)


def kernel(
    emb_hbm, cl_hbm, rk_hbm, out_ref,
    emb, cl, rk, buf, send, onehot, meta_send, meta_recv, rank_lane, rank_sub, lane_acc, sub_acc,
    part_send, part_recv, final, back_recv,
    in_s, meta_s, meta_r, own_s, own_r, rank_s, rank_r, part_s, part_r, back_s, back_r,
    *, groups, members, slot,
):
    rows, depth = emb.shape
    slots = groups * slot
    tiles = slots // 128
    chips = members // 2
    group, member = lax.axis_index("grp"), lax.axis_index("blk")
    chip, core = member // 2, lax.rem(member, 2)
    after, before = lax.rem(chip + 1, chips), lax.rem(chip + chips - 1, chips)
    partner = {"blk": chip * 2 + 1 - core}
    next_same, next_other = {"blk": after * 2 + core}, {"blk": after * 2 + 1 - core}
    prev_same, prev_other = {"blk": before * 2 + core}, {"blk": before * 2 + 1 - core}
    gz, gx = group // 4, lax.rem(group, 4)

    fetch = [
        pltpu.make_async_copy(cl_hbm, cl, in_s.at[0]),
        pltpu.make_async_copy(emb_hbm, emb, in_s.at[1]),
        pltpu.make_async_copy(rk_hbm, rk, in_s.at[2]),
    ]
    for c in fetch:
        c.start()

    def group_at(k, sign):
        dz, dx = STEPS[k]
        dz, dx = (sign * dz) % 4, (sign * dx) % 4
        return lax.rem(gz + dz, 4) * 4 + lax.rem(gx + dx, 4)

    def ahead(k):
        return {"grp": group_at(k, 1)}

    def behind(k):
        return {"grp": group_at(k, -1)}

    barrier = pltpu.get_barrier_semaphore()
    for k in range(1, groups):
        pl.semaphore_signal(barrier, inc=1, device_id=ahead(k), device_id_type=MESH)
    for peer in (partner, next_same, next_other, prev_same, prev_other):
        pl.semaphore_signal(barrier, inc=1, device_id=peer, device_id_type=MESH)

    def copy(src, dst, ssem, rsem, peer):
        return pltpu.make_async_remote_copy(
            src_ref=src, dst_ref=dst, send_sem=ssem, recv_sem=rsem,
            device_id=peer, device_id_type=MESH,
        )

    def piece(k):
        return pl.ds(k * slot, slot)

    def exchange(k):
        return copy(send.at[piece(k)], buf.at[OWN, piece(k)], own_s.at[OWN], own_r.at[OWN, k], ahead(k))

    def to_partner(k):
        return copy(buf.at[OWN, piece(k)], buf.at[PARTNER, piece(k)], own_s.at[PARTNER], own_r.at[PARTNER, k], partner)

    def to_prev(k):
        return copy(buf.at[OWN, piece(k)], buf.at[NEXT, piece(k)], own_s.at[NEXT], own_r.at[NEXT, k], prev_same)

    def to_next(k):
        return copy(buf.at[OWN, piece(k)], buf.at[PREV, piece(k)], own_s.at[PREV], own_r.at[PREV, k], next_same)

    def across(k):
        return copy(buf.at[NEXT, piece(k)], buf.at[CROSS, piece(k)], own_s.at[CROSS], own_r.at[CROSS, k], partner)

    def meta(k):
        return copy(meta_send.at[k], meta_recv.at[k], meta_s, meta_r.at[k], ahead(k))

    lines = lax.broadcasted_iota(jnp.int32, (groups, rows), 0)
    owner = jnp.full((groups, rows), group, jnp.int32)
    for k in range(1, groups):
        owner = jnp.where(lines == k, group_at(k, 1), owner)
    earlier = lax.broadcasted_iota(jnp.int32, (rows, rows), 0) < lax.broadcasted_iota(jnp.int32, (rows, rows), 1)
    earlier = jnp.where(earlier, 1.0, 0.0).astype(jnp.bfloat16)
    fetch[0].wait()
    mine = lax.bitwise_and(cl[...], groups - 1) == owner
    count = jnp.dot(
        jnp.where(mine, 1.0, 0.0).astype(jnp.bfloat16), earlier, preferred_element_type=jnp.float32
    )
    target = jnp.sum(
        jnp.where(mine, count + (lines * slot).astype(jnp.float32), 0.0), axis=0, keepdims=True
    )
    part = 4 * slot

    def place(j):
        at = (lax.broadcasted_iota(jnp.int32, (part, rows), 0) + j * part).astype(jnp.float32)
        onehot[j * part : (j + 1) * part, :] = jnp.where(at == target, 1.0, 0.0).astype(jnp.bfloat16)

    def pack(j):
        return jnp.dot(
            onehot[j * part : (j + 1) * part, :], unit, preferred_element_type=jnp.float32
        ).astype(jnp.bfloat16)

    place(0)
    fetch[1].wait()
    values = emb[...].astype(jnp.float32)
    squares = jnp.sum(values * values, axis=1, keepdims=True)
    unit = (values * lax.rsqrt(squares + epsilon)).astype(jnp.bfloat16)
    packed = pack(0)
    buf[OWN, 0:slot, :] = packed[0:slot]
    send[0:part, :] = packed
    pl.semaphore_wait(barrier, groups - 1 + 5)
    to_prev(0).start()
    to_next(0).start()
    for k in range(1, 4):
        exchange(k).start()
    to_partner(0).start()

    for j in range(1, slots // part):
        place(j)
    fetch[2].wait()
    rank = rk[...]
    line8 = lax.broadcasted_iota(jnp.int32, (8, rows), 0)
    high = lax.shift_right_logical(rank, 8).astype(jnp.float32)
    low = lax.bitwise_and(rank, 255).astype(jnp.float32)
    table = jnp.where(line8 == 0, high, jnp.where(line8 == 1, low, 1.0)).astype(jnp.bfloat16)
    found = lax.dot_general(
        table, onehot[...], (((1,), (1,)), ((), ())), preferred_element_type=jnp.float32
    )
    spot = found[0:1] * 256.0 + found[1:2] + (1.0 - found[2:3]) * FAR
    left = lax.broadcasted_iota(jnp.int32, (8, 128), 1) < slot
    for t in range(tiles):
        tile = jnp.broadcast_to(spot[:, t * 128 : (t + 1) * 128], (8, 128))
        turned = pltpu.roll(tile, slot, 1)
        meta_send[2 * t] = jnp.where(left, tile, turned)
        meta_send[2 * t + 1] = jnp.where(left, turned, tile)
    for k in range(1, groups):
        meta(k).start()
    for j in range(1, slots // part):
        send[j * part : (j + 1) * part, :] = pack(j)
        for k in range(4 * j, 4 * j + 4):
            exchange(k).start()

    lane_acc[...] = jnp.full(lane_acc.shape, -1.0, jnp.float32)
    sub_acc[...] = jnp.full(sub_acc.shape, -1.0, jnp.float32)

    rank_copies = [
        copy(rank_lane.at[OWN], rank_lane.at[PARTNER], rank_s.at[PARTNER], rank_r.at[PARTNER], partner),
        copy(rank_lane.at[OWN], rank_lane.at[NEXT], rank_s.at[NEXT], rank_r.at[NEXT], prev_same),
        copy(rank_lane.at[OWN], rank_lane.at[PREV], rank_s.at[PREV], rank_r.at[PREV], next_same),
        copy(rank_lane.at[NEXT], rank_lane.at[CROSS], rank_s.at[CROSS], rank_r.at[CROSS], partner),
    ]

    def spread(which, into):
        for t in range(tiles):
            tile = jnp.broadcast_to(rank_lane[which, t : t + 1, :], (128, 128))
            rank_sub[into, t * 128 : (t + 1) * 128, :] = jnp.transpose(tile)

    def relay(k):
        to_prev(k).wait_recv()
        across(k).start()

    def score(x, x0, size, y, y0, width, subs, lanes):
        at = pl.ds(x0, size)
        here = rank_sub[subs, at, :]
        best = jnp.full((size, 128), -1.0, jnp.float32)
        s = lax.dot_general(
            buf[x, at, :], buf[y, pl.ds(y0, width), :], (((1,), (1,)), ((), ())),
            preferred_element_type=jnp.float32,
        )
        for h in range(width // 128):
            t = y0 // 128 + h
            sh = s[:, h * 128 : (h + 1) * 128]
            there = rank_lane[y, pl.ds(t, 1), :]
            best = jnp.maximum(best, jnp.where(there < here, sh, -1.0))
            if lanes is not None:
                up = jnp.where(here < there, sh, -1.0)
                lane_acc[lanes, t] = jnp.maximum(lane_acc[lanes, t], jnp.max(up.reshape(size // 8, 8, 128), axis=0))
        sub_acc[subs, at, :] = jnp.maximum(sub_acc[subs, at, :], best)

    def each(first, last, body):
        def step(i, carry):
            body(i)
            return carry
        lax.fori_loop(first, last, step, 0)

    far = NEXT + chip // (chips // 2)

    def chunk(i):
        return pl.multiple_of(i * part, part)

    for k in range(1, groups):
        exchange(k).wait_recv()
        to_prev(k).start()
        to_next(k).start()
        to_partner(k).start()
        if k >= LAG:
            relay(k - LAG)
        if k == 4:
            for i in range(1, groups):
                meta(i).wait_recv()
            for t in range(tiles):
                first = meta_send[0] if t == 0 else meta_recv[2 * t]
                rank_lane[OWN, t : t + 1, :] = jnp.where(left, first, meta_recv[2 * t + 1])[0:1]
            for c in rank_copies[:3]:
                c.start()
            spread(OWN, 0)
        if k == 8:
            for c in rank_copies[:3]:
                c.wait_recv()
            rank_copies[3].start()
            spread(PREV, 1)
        if k == 9:
            for j in range(2):
                score(OWN, 0, (j + 1) * part, OWN, j * part, part, 0, 0)
        if k == 10:
            for i in range(8):
                to_partner(i).wait_recv()
            each(0, 2, lambda i: score(OWN, 0, 2 * part, PARTNER, chunk(i), part, 0, None))
        if k == 13:
            score(OWN, 0, 3 * part, OWN, 2 * part, part, 0, 0)

    score(OWN, 0, slots, OWN, 3 * part, part, 0, 0)
    relay(16 - LAG)
    each(0, 2, lambda i: score(OWN, 2 * part, 2 * part, PARTNER, chunk(i), part, 0, None))
    for i in range(8, 16):
        to_partner(i).wait_recv()
    relay(17 - LAG)
    each(2, 4, lambda i: score(OWN, 0, slots, PARTNER, chunk(i), part, 0, None))
    rank_copies[3].wait_recv()

    sent = 18 - LAG
    for j in range(slots // part):
        now = j * part
        while sent < 4 * j + 4:
            relay(sent)
            sent += 1
        score(OWN, 0, slots, NEXT, now, part, 0, NEXT)
        for k in range(4 * j, 4 * j + 4):
            across(k).wait_recv()
            to_next(k).wait_recv()
        score(OWN, 0, slots, CROSS, now, part, 0, CROSS)
        if j == 1:
            each(0, 2, lambda i: score(PREV, 0, 2 * part, far, chunk(i), part, 1, far))
        if j >= 2:
            score(PREV, 0, now + part, far, now, part, 1, far)
            each(0, j, lambda i: score(PREV, now, part, far, chunk(i), part, 1, far))

    for t in range(tiles):
        line = slice(t, t + 1)
        for i, which in enumerate((NEXT, CROSS)):
            part_send[i, line, :] = jnp.max(lane_acc[which, t], axis=0, keepdims=True)
        tile = jnp.transpose(sub_acc[1, t * 128 : (t + 1) * 128, :])
        part_send[2, line, :] = jnp.max(tile, axis=0, keepdims=True)
    part_copies = [
        copy(part_send.at[i], part_recv.at[i], part_s.at[i], part_r.at[i], peer)
        for i, peer in enumerate((next_same, next_other, prev_same))
    ]
    for c in part_copies:
        c.start()
    for t in range(tiles):
        tile = jnp.maximum(jnp.transpose(sub_acc[0, t * 128 : (t + 1) * 128, :]), jnp.max(lane_acc[0, t], axis=0, keepdims=True))
        final[t : t + 1, :] = jnp.max(tile, axis=0, keepdims=True)
    for c in part_copies:
        c.wait_recv()
    final[...] = jnp.maximum(
        jnp.maximum(final[...], part_recv[0]), jnp.maximum(part_recv[1], part_recv[2])
    )

    def back(k):
        return copy(final, back_recv.at[k], back_s, back_r.at[k], behind(k))

    for k in range(1, groups):
        back(k).start()
    for k in range(1, groups):
        back(k).wait_recv()
    found = []
    for t in range(tiles):
        line = slice(t, t + 1)
        first = final[line, :] if t == 0 else back_recv[2 * t, line, :]
        found.append(jnp.where(left[0:1], first, back_recv[2 * t + 1, line, :]))
    got = jnp.concatenate(found, axis=1)
    one = got.astype(jnp.bfloat16).astype(jnp.float32)
    rest = got - one
    two = rest.astype(jnp.bfloat16).astype(jnp.float32)
    line8 = lax.broadcasted_iota(jnp.int32, (8, slots), 0)
    terms = jnp.where(
        line8 == 0, one, jnp.where(line8 == 1, two, jnp.where(line8 == 2, rest - two, 0.0))
    ).astype(jnp.bfloat16)
    out = jnp.dot(terms, onehot[...], preferred_element_type=jnp.float32)
    out_ref[...] = jnp.sum(out, axis=0, keepdims=True)

    copy(send.at[slot:slots], buf.at[OWN, slot:slots], own_s.at[OWN], own_r.at[OWN, 1], partner).wait_send()
    for which in (PARTNER, NEXT, PREV, CROSS):
        copy(buf.at[OWN], buf.at[which], own_s.at[which], own_r.at[which, 0], partner).wait_send()
    copy(meta_send.at[1:groups], meta_recv.at[1:groups], meta_s, meta_r.at[1], partner).wait_send()
    for c in rank_copies + part_copies:
        c.wait_send()
    copy(meta_send.at[1:groups], back_recv.at[1:groups], back_s, back_r.at[1], partner).wait_send()


def local(embeddings, cluster_ids, rank_key):
    rows, depth = embeddings.shape
    groups, members = lax.axis_size("grp"), lax.axis_size("blk")
    slot = 2 * rows // groups
    slots = groups * slot
    dma = pltpu.SemaphoreType.DMA
    out = pl.pallas_call(
        functools.partial(kernel, groups=groups, members=members, slot=slot),
        out_shape=jax.ShapeDtypeStruct((1, rows), jnp.float32),
        in_specs=[pl.BlockSpec(memory_space=pltpu.HBM)] * 3,
        out_specs=pl.BlockSpec(memory_space=pltpu.VMEM),
        scratch_shapes=[
            pltpu.VMEM((rows, depth), jnp.bfloat16),
            pltpu.VMEM((1, rows), jnp.int32),
            pltpu.VMEM((1, rows), jnp.int32),
            pltpu.VMEM((5, slots, depth), jnp.bfloat16),
            pltpu.VMEM((slots, depth), jnp.bfloat16),
            pltpu.VMEM((slots, rows), jnp.bfloat16),
            pltpu.VMEM((groups, 8, 128), jnp.float32),
            pltpu.VMEM((groups, 8, 128), jnp.float32),
            pltpu.VMEM((5, slots // 128, 128), jnp.float32),
            pltpu.VMEM((2, slots, 128), jnp.float32),
            pltpu.VMEM((4, slots // 128, 8, 128), jnp.float32),
            pltpu.VMEM((2, slots, 128), jnp.float32),
            pltpu.VMEM((3, slots // 128, 128), jnp.float32),
            pltpu.VMEM((3, slots // 128, 128), jnp.float32),
            pltpu.VMEM((slots // 128, 128), jnp.float32),
            pltpu.VMEM((groups, slots // 128, 128), jnp.float32),
            dma((3,)),
            dma, dma((groups,)),
            dma((5,)), dma((5, groups)),
            dma((5,)), dma((5,)),
            dma((3,)), dma((3,)),
            dma, dma((groups,)),
        ],
        compiler_params=pltpu.CompilerParams(
            collective_id=0, has_side_effects=True, vmem_limit_bytes=48 * 1024 * 1024
        ),
    )(embeddings, cluster_ids.reshape(1, rows), rank_key.reshape(1, rows))
    return out.reshape(rows)


def solution(mesh):
    placed = (P(("grp", "blk"), None), P(("grp", "blk")), P(("grp", "blk")))
    return jax.shard_map(
        local, mesh=mesh, in_specs=placed, out_specs=P(("grp", "blk")), check_vma=False
    )
```

time: 84.1 us -> 74.2 us (0.88)
  Pallas kernels: 80.6 us -> 70.7 us
    pallas_call x1, Pallas kernels: 80.6 us -> 70.7 us  [local(): pl.pallas_call(functools.partial(kernel, groups=groups, members=members,...]
where the time goes in v2:
time: 74.2 us; the launch traced here: 73.9 us
  Pallas kernels  70.7 us (95%)
  local copies, waits for them, and re-layouts  3.17 us (4%)
    pallas_call x1, Pallas kernels, local(): pl.pallas_call(functools.partial(kernel, groups=groups, members=members,...  70.7 us
    unnamed x7, local copies, waits for them, and re-layouts  3.17 us

profile of v2, /device:TPU:0, one launch (start us, length us, event | category | flops | bytes accessed | tf_op | source)
XLA Modules:
  0.0 73.9 jit_solution(9297139647973709050)
XLA Ops:
  0.0 0.0 copy-start.1
  0.0 0.7 copy-done.1
  0.7 0.0 copy-start
  0.7 1.2 %copy-done = bf16[512,1024]{1,0:T(8,128)(2,1)S(1)} copy-done((bf16[512,1024]{1,0:T(8,128)(2,1)S(1)}, bf16[512,1024]{1,0:T(8,128)(2,1)}, u32[]{:S(2)}) %copy-start) | copy-done | bytes 1048600
  1.9 0.0 copy-start.2
  1.9 0.7 copy-done.2
  2.6 70.7 %shard_map.37 = f32[1,512]{1,0:T(1,128)S(1)} custom-call(bf16[512,1024]{1,0:T(8,128)(2,1)S(1)} %copy-done, s32[1,512]{1,0:T(1,128)S(1)} %bitcast.4, s32[1,512]{1,0:T(1,128)S(1)} %bitcast.5), custom_call_target="tpu_custom_call" | custom-call | tf_op jit(solution)/shard_map/pallas_call | solution.py:323
  73.3 0.6 copy.5
Async XLA Ops:
  0.0 0.7 copy-start.1
  0.7 1.2 %copy-start = (bf16[512,1024]{1,0:T(8,128)(2,1)S(1)}, bf16[512,1024]{1,0:T(8,128)(2,1)}, u32[]{:S(2)}) copy-start(bf16[512,1024]{1,0:T(8,128)(2,1)} %emb_hbm.1) | copy-start | bytes 3145732
  1.9 0.7 copy-start.2

commit v3 on v2

--- a/solution.py
+++ b/solution.py
@@ -10,8 +10,7 @@
 MESH = pl.DeviceIdType.MESH
 epsilon = 1e-06
 FAR = 1.0e6
-OWN, PARTNER, NEXT, CROSS, PREV = range(5)
-LAG = 6
+OWN, PARTNER, NEXT, PREV = range(4)
 
 
 STEPS = (
@@ -23,8 +22,8 @@
 def kernel(
     emb_hbm, cl_hbm, rk_hbm, out_ref,
     emb, cl, rk, buf, send, onehot, meta_send, meta_recv, rank_lane, rank_sub, lane_acc, sub_acc,
-    part_send, part_recv, final, back_recv,
-    in_s, meta_s, meta_r, own_s, own_r, rank_s, rank_r, part_s, part_r, back_s, back_r,
+    result, returned,
+    in_s, meta_s, meta_r, own_s, own_r, rank_s, rank_r, back_s, back_r,
     *, groups, members, slot,
 ):
     rows, depth = emb.shape
@@ -36,6 +35,9 @@
     after, before = lax.rem(chip + 1, chips), lax.rem(chip + chips - 1, chips)
     partner = {"blk": chip * 2 + 1 - core}
     next_same, next_other = {"blk": after * 2 + core}, {"blk": after * 2 + 1 - core}
+    crossed = after // (chips // 2)
+    next_seen = {"blk": after * 2 + lax.rem(core + crossed, 2)}
+    prev_seen = {"blk": before * 2 + lax.rem(core + chip // (chips // 2), 2)}
     prev_same, prev_other = {"blk": before * 2 + core}, {"blk": before * 2 + 1 - core}
     gz, gx = group // 4, lax.rem(group, 4)
 
@@ -83,10 +85,7 @@
         return copy(buf.at[OWN, piece(k)], buf.at[NEXT, piece(k)], own_s.at[NEXT], own_r.at[NEXT, k], prev_same)
 
     def to_next(k):
-        return copy(buf.at[OWN, piece(k)], buf.at[PREV, piece(k)], own_s.at[PREV], own_r.at[PREV, k], next_same)
-
-    def across(k):
-        return copy(buf.at[NEXT, piece(k)], buf.at[CROSS, piece(k)], own_s.at[CROSS], own_r.at[CROSS, k], partner)
+        return copy(buf.at[OWN, piece(k)], buf.at[PREV, piece(k)], own_s.at[PREV], own_r.at[PREV, k], next_seen)
 
     def meta(k):
         return copy(meta_send.at[k], meta_recv.at[k], meta_s, meta_r.at[k], ahead(k))
@@ -162,22 +161,17 @@
     rank_copies = [
         copy(rank_lane.at[OWN], rank_lane.at[PARTNER], rank_s.at[PARTNER], rank_r.at[PARTNER], partner),
         copy(rank_lane.at[OWN], rank_lane.at[NEXT], rank_s.at[NEXT], rank_r.at[NEXT], prev_same),
-        copy(rank_lane.at[OWN], rank_lane.at[PREV], rank_s.at[PREV], rank_r.at[PREV], next_same),
-        copy(rank_lane.at[NEXT], rank_lane.at[CROSS], rank_s.at[CROSS], rank_r.at[CROSS], partner),
+        copy(rank_lane.at[OWN], rank_lane.at[PREV], rank_s.at[PREV], rank_r.at[PREV], next_seen),
     ]
 
-    def spread(which, into):
+    def spread(which):
         for t in range(tiles):
             tile = jnp.broadcast_to(rank_lane[which, t : t + 1, :], (128, 128))
-            rank_sub[into, t * 128 : (t + 1) * 128, :] = jnp.transpose(tile)
-
-    def relay(k):
-        to_prev(k).wait_recv()
-        across(k).start()
-
-    def score(x, x0, size, y, y0, width, subs, lanes):
+            rank_sub[which, t * 128 : (t + 1) * 128, :] = jnp.transpose(tile)
+
+    def score(x, x0, size, y, y0, width):
         at = pl.ds(x0, size)
-        here = rank_sub[subs, at, :]
+        here = rank_sub[x, at, :]
         best = jnp.full((size, 128), -1.0, jnp.float32)
         s = lax.dot_general(
             buf[x, at, :], buf[y, pl.ds(y0, width), :], (((1,), (1,)), ((), ())),
@@ -188,10 +182,9 @@
             sh = s[:, h * 128 : (h + 1) * 128]
             there = rank_lane[y, pl.ds(t, 1), :]
             best = jnp.maximum(best, jnp.where(there < here, sh, -1.0))
-            if lanes is not None:
-                up = jnp.where(here < there, sh, -1.0)
-                lane_acc[lanes, t] = jnp.maximum(lane_acc[lanes, t], jnp.max(up.reshape(size // 8, 8, 128), axis=0))
-        sub_acc[subs, at, :] = jnp.maximum(sub_acc[subs, at, :], best)
+            up = jnp.where(here < there, sh, -1.0)
+            lane_acc[y, t] = jnp.maximum(lane_acc[y, t], jnp.max(up.reshape(size // 8, 8, 128), axis=0))
+        sub_acc[x, at, :] = jnp.maximum(sub_acc[x, at, :], best)
 
     def each(first, last, body):
         def step(i, carry):
@@ -199,8 +192,6 @@
             return carry
         lax.fori_loop(first, last, step, 0)
 
-    far = NEXT + chip // (chips // 2)
-
     def chunk(i):
         return pl.multiple_of(i * part, part)
 
@@ -209,91 +200,101 @@
         to_prev(k).start()
         to_next(k).start()
         to_partner(k).start()
-        if k >= LAG:
-            relay(k - LAG)
         if k == 4:
             for i in range(1, groups):
                 meta(i).wait_recv()
             for t in range(tiles):
                 first = meta_send[0] if t == 0 else meta_recv[2 * t]
                 rank_lane[OWN, t : t + 1, :] = jnp.where(left, first, meta_recv[2 * t + 1])[0:1]
-            for c in rank_copies[:3]:
+            for c in rank_copies:
                 c.start()
-            spread(OWN, 0)
-        if k == 8:
-            for c in rank_copies[:3]:
+            spread(OWN)
+        if k == 10:
+            for c in rank_copies:
                 c.wait_recv()
-            rank_copies[3].start()
-            spread(PREV, 1)
-        if k == 9:
-            for j in range(2):
-                score(OWN, 0, (j + 1) * part, OWN, j * part, part, 0, 0)
-        if k == 10:
-            for i in range(8):
-                to_partner(i).wait_recv()
-            each(0, 2, lambda i: score(OWN, 0, 2 * part, PARTNER, chunk(i), part, 0, None))
-        if k == 13:
-            score(OWN, 0, 3 * part, OWN, 2 * part, part, 0, 0)
-
-    score(OWN, 0, slots, OWN, 3 * part, part, 0, 0)
-    relay(16 - LAG)
-    each(0, 2, lambda i: score(OWN, 2 * part, 2 * part, PARTNER, chunk(i), part, 0, None))
-    for i in range(8, 16):
-        to_partner(i).wait_recv()
-    relay(17 - LAG)
-    each(2, 4, lambda i: score(OWN, 0, slots, PARTNER, chunk(i), part, 0, None))
-    rank_copies[3].wait_recv()
-
-    sent = 18 - LAG
+            spread(PARTNER)
+
     for j in range(slots // part):
+        score(OWN, 0, (j + 1) * part, OWN, j * part, part)
+    spread(PREV)
+    for k in range(groups):
+        to_partner(k).wait_recv()
+    each(0, 2, lambda i: score(core, 0, slots, 1 - core, pl.multiple_of(core * 2 * part + i * part, part), part))
+
+    last = slots // part - 1
+    for j in range(last):
         now = j * part
-        while sent < 4 * j + 4:
-            relay(sent)
-            sent += 1
-        score(OWN, 0, slots, NEXT, now, part, 0, NEXT)
         for k in range(4 * j, 4 * j + 4):
-            across(k).wait_recv()
+            to_prev(k).wait_recv()
+        score(OWN, 0, slots, NEXT, now, part)
+        score(PARTNER, 0, slots, NEXT, now, part)
+        for k in range(4 * j, 4 * j + 4):
             to_next(k).wait_recv()
-        score(OWN, 0, slots, CROSS, now, part, 0, CROSS)
         if j == 1:
-            each(0, 2, lambda i: score(PREV, 0, 2 * part, far, chunk(i), part, 1, far))
+            each(0, 2, lambda i: score(PREV, 0, 2 * part, NEXT, chunk(i), part))
         if j >= 2:
-            score(PREV, 0, now + part, far, now, part, 1, far)
-            each(0, j, lambda i: score(PREV, now, part, far, chunk(i), part, 1, far))
-
-    for t in range(tiles):
-        line = slice(t, t + 1)
-        for i, which in enumerate((NEXT, CROSS)):
-            part_send[i, line, :] = jnp.max(lane_acc[which, t], axis=0, keepdims=True)
-        tile = jnp.transpose(sub_acc[1, t * 128 : (t + 1) * 128, :])
-        part_send[2, line, :] = jnp.max(tile, axis=0, keepdims=True)
-    part_copies = [
-        copy(part_send.at[i], part_recv.at[i], part_s.at[i], part_r.at[i], peer)
-        for i, peer in enumerate((next_same, next_other, prev_same))
-    ]
-    for c in part_copies:
-        c.start()
-    for t in range(tiles):
-        tile = jnp.maximum(jnp.transpose(sub_acc[0, t * 128 : (t + 1) * 128, :]), jnp.max(lane_acc[0, t], axis=0, keepdims=True))
-        final[t : t + 1, :] = jnp.max(tile, axis=0, keepdims=True)
-    for c in part_copies:
-        c.wait_recv()
-    final[...] = jnp.maximum(
-        jnp.maximum(final[...], part_recv[0]), jnp.maximum(part_recv[1], part_recv[2])
-    )
-
-    def back(k):
-        return copy(final, back_recv.at[k], back_s, back_r.at[k], behind(k))
-
-    for k in range(1, groups):
-        back(k).start()
-    for k in range(1, groups):
-        back(k).wait_recv()
+            score(PREV, now, part, NEXT, 0, now)
+            score(PREV, 0, now + part, NEXT, now, part)
+
+    def gather(which, t):
+        tile = jnp.transpose(sub_acc[which, t * 128 : (t + 1) * 128, :])
+        return jnp.max(tile, axis=0, keepdims=True)
+
+    def along(which, t):
+        return jnp.max(lane_acc[which, t], axis=0, keepdims=True)
+
+    homes = {PREV: prev_seen, PARTNER: partner, NEXT: next_same, OWN: {}}
+
+    def back(which, k):
+        return copy(
+            result.at[which, k // 2], returned.at[which, k], back_s.at[which], back_r.at[which],
+            {**behind(k), **homes[which]},
+        )
+
+    def send_back(which):
+        for k in range(1 if which == OWN else 0, groups):
+            back(which, k).start()
+
+    now = last * part
+    for k in range(4 * last, 4 * last + 4):
+        to_next(k).wait_recv()
+    for k in range(4 * last, 4 * last + 4):
+        to_prev(k).wait_recv()
+    score(PREV, now, part, NEXT, 0, now)
+    score(PREV, 0, now + part, NEXT, now, part)
+    for t in range(tiles):
+        result[PREV, t] = gather(PREV, t)
+    score(PARTNER, 0, slots, NEXT, now, part)
+    send_back(PREV)
+    for t in range(tiles):
+        result[PARTNER, t] = jnp.maximum(gather(PARTNER, t), along(PARTNER, t))
+    score(OWN, 0, slots, NEXT, now, part)
+    for t in range(tiles):
+        result[NEXT, t] = along(NEXT, t)
+    send_back(NEXT)
+    send_back(PARTNER)
+    for t in range(tiles):
+        result[OWN, t] = jnp.maximum(gather(OWN, t), along(OWN, t))
+    send_back(OWN)
+
+    def all_back(which):
+        first = 1 if which == OWN else 0
+        return copy(
+            returned.at[which, first:groups], returned.at[which, first:groups],
+            back_s.at[which], back_r.at[which], partner,
+        )
+
+    for which in (OWN, PARTNER, NEXT, PREV):
+        all_back(which).wait_recv()
     found = []
     for t in range(tiles):
-        line = slice(t, t + 1)
-        first = final[line, :] if t == 0 else back_recv[2 * t, line, :]
-        found.append(jnp.where(left[0:1], first, back_recv[2 * t + 1, line, :]))
+        pair = []
+        for k in (2 * t, 2 * t + 1):
+            one = result[OWN, 0] if k == 0 else returned[OWN, k]
+            for which in (PARTNER, NEXT, PREV):
+                one = jnp.maximum(one, returned[which, k])
+            pair.append(one)
+        found.append(jnp.where(left[0:1], pair[0], pair[1]))
     got = jnp.concatenate(found, axis=1)
     one = got.astype(jnp.bfloat16).astype(jnp.float32)
     rest = got - one
@@ -306,12 +307,13 @@
     out_ref[...] = jnp.sum(out, axis=0, keepdims=True)
 
     copy(send.at[slot:slots], buf.at[OWN, slot:slots], own_s.at[OWN], own_r.at[OWN, 1], partner).wait_send()
-    for which in (PARTNER, NEXT, PREV, CROSS):
+    for which in (PARTNER, NEXT, PREV):
         copy(buf.at[OWN], buf.at[which], own_s.at[which], own_r.at[which, 0], partner).wait_send()
     copy(meta_send.at[1:groups], meta_recv.at[1:groups], meta_s, meta_r.at[1], partner).wait_send()
-    for c in rank_copies + part_copies:
+    for c in rank_copies:
         c.wait_send()
-    copy(meta_send.at[1:groups], back_recv.at[1:groups], back_s, back_r.at[1], partner).wait_send()
+    for which in (OWN, PARTNER, NEXT, PREV):
+        all_back(which).wait_send()
 
 
 def local(embeddings, cluster_ids, rank_key):
@@ -329,25 +331,22 @@
             pltpu.VMEM((rows, depth), jnp.bfloat16),
             pltpu.VMEM((1, rows), jnp.int32),
             pltpu.VMEM((1, rows), jnp.int32),
-            pltpu.VMEM((5, slots, depth), jnp.bfloat16),
+            pltpu.VMEM((4, slots, depth), jnp.bfloat16),
             pltpu.VMEM((slots, depth), jnp.bfloat16),
             pltpu.VMEM((slots, rows), jnp.bfloat16),
             pltpu.VMEM((groups, 8, 128), jnp.float32),
             pltpu.VMEM((groups, 8, 128), jnp.float32),
-            pltpu.VMEM((5, slots // 128, 128), jnp.float32),
-            pltpu.VMEM((2, slots, 128), jnp.float32),
+            pltpu.VMEM((4, slots // 128, 128), jnp.float32),
+            pltpu.VMEM((4, slots, 128), jnp.float32),
             pltpu.VMEM((4, slots // 128, 8, 128), jnp.float32),
-            pltpu.VMEM((2, slots, 128), jnp.float32),
-            pltpu.VMEM((3, slots // 128, 128), jnp.float32),
-            pltpu.VMEM((3, slots // 128, 128), jnp.float32),
-            pltpu.VMEM((slots // 128, 128), jnp.float32),
-            pltpu.VMEM((groups, slots // 128, 128), jnp.float32),
+            pltpu.VMEM((4, slots, 128), jnp.float32),
+            pltpu.VMEM((4, slots // 128, 1, 128), jnp.float32),
+            pltpu.VMEM((4, groups, 1, 128), jnp.float32),
             dma((3,)),
             dma, dma((groups,)),
-            dma((5,)), dma((5, groups)),
-            dma((5,)), dma((5,)),
-            dma((3,)), dma((3,)),
-            dma, dma((groups,)),
+            dma((4,)), dma((4, groups)),
+            dma((4,)), dma((4,)),
+            dma((4,)), dma((4,)),
         ],
         compiler_params=pltpu.CompilerParams(
             collective_id=0, has_side_effects=True, vmem_limit_bytes=48 * 1024 * 1024

time: 74.2 us -> 70.9 us (0.956)
  Pallas kernels: 70.7 us -> 67.5 us
    pallas_call x1, Pallas kernels: 70.7 us -> 67.5 us  [local(): pl.pallas_call(functools.partial(kernel, groups=groups, members=members,...]
where the time goes in v3:
time: 70.9 us; the launch traced here: 70.7 us
  Pallas kernels  67.5 us (95%)
  local copies, waits for them, and re-layouts  3.17 us (4%)
    pallas_call x1, Pallas kernels, local(): pl.pallas_call(functools.partial(kernel, groups=groups, members=members,...  67.5 us
    unnamed x7, local copies, waits for them, and re-layouts  3.17 us

profile of v3, /device:TPU:0, one launch (start us, length us, event | category | flops | bytes accessed | tf_op | source)
XLA Modules:
  0.0 70.7 jit_solution(6705398015826142540)
XLA Ops:
  0.0 0.0 copy-start.1
  0.0 0.7 copy-done.1
  0.7 0.0 copy-start
  0.7 1.2 %copy-done = bf16[512,1024]{1,0:T(8,128)(2,1)S(1)} copy-done((bf16[512,1024]{1,0:T(8,128)(2,1)S(1)}, bf16[512,1024]{1,0:T(8,128)(2,1)}, u32[]{:S(2)}) %copy-start) | copy-done | bytes 1048600
  1.9 0.0 copy-start.2
  1.9 0.7 copy-done.2
  2.6 67.5 %shard_map.37 = f32[1,512]{1,0:T(1,128)S(1)} custom-call(bf16[512,1024]{1,0:T(8,128)(2,1)S(1)} %copy-done, s32[1,512]{1,0:T(1,128)S(1)} %bitcast.4, s32[1,512]{1,0:T(1,128)S(1)} %bitcast.5), custom_call_target="tpu_custom_call" | custom-call | tf_op jit(solution)/shard_map/pallas_call | solution.py:325
  70.1 0.6 copy.5
Async XLA Ops:
  0.0 0.7 copy-start.1
  0.7 1.2 %copy-start = (bf16[512,1024]{1,0:T(8,128)(2,1)S(1)}, bf16[512,1024]{1,0:T(8,128)(2,1)}, u32[]{:S(2)}) copy-start(bf16[512,1024]{1,0:T(8,128)(2,1)} %emb_hbm.1) | copy-start | bytes 3145732
  1.9 0.7 copy-start.2

commit v4 on v3

--- a/solution.py
+++ b/solution.py
@@ -11,6 +11,7 @@
 epsilon = 1e-06
 FAR = 1.0e6
 OWN, PARTNER, NEXT, PREV = range(4)
+EARLY, CUT = 2, 2
 
 
 STEPS = (
@@ -23,7 +24,7 @@
     emb_hbm, cl_hbm, rk_hbm, out_ref,
     emb, cl, rk, buf, send, onehot, meta_send, meta_recv, rank_lane, rank_sub, lane_acc, sub_acc,
     result, returned,
-    in_s, meta_s, meta_r, own_s, own_r, rank_s, rank_r, back_s, back_r,
+    in_s, meta_s, meta_r, own_s, own_r, rank_s, rank_r, back_s, back_r, early_r,
     *, groups, members, slot,
 ):
     rows, depth = emb.shape
@@ -78,6 +79,18 @@
     def exchange(k):
         return copy(send.at[piece(k)], buf.at[OWN, piece(k)], own_s.at[OWN], own_r.at[OWN, k], ahead(k))
 
+    def some(k, i):
+        return pl.ds(k * slot + i * (slot // CUT), slot // CUT)
+
+    def exchange_some(k, i):
+        return copy(send.at[some(k, i)], buf.at[OWN, some(k, i)], own_s.at[OWN], early_r.at[k, i], ahead(k))
+
+    def to_prev_some(k, i):
+        return copy(buf.at[OWN, some(k, i)], buf.at[NEXT, some(k, i)], own_s.at[NEXT], own_r.at[NEXT, k], prev_same)
+
+    def to_next_some(k, i):
+        return copy(buf.at[OWN, some(k, i)], buf.at[PREV, some(k, i)], own_s.at[PREV], own_r.at[PREV, k], next_seen)
+
     def to_partner(k):
         return copy(buf.at[OWN, piece(k)], buf.at[PARTNER, piece(k)], own_s.at[PARTNER], own_r.at[PARTNER, k], partner)
 
@@ -97,6 +110,7 @@
     earlier = lax.broadcasted_iota(jnp.int32, (rows, rows), 0) < lax.broadcasted_iota(jnp.int32, (rows, rows), 1)
     earlier = jnp.where(earlier, 1.0, 0.0).astype(jnp.bfloat16)
     fetch[0].wait()
+    fetch[1].wait()
     mine = lax.bitwise_and(cl[...], groups - 1) == owner
     count = jnp.dot(
         jnp.where(mine, 1.0, 0.0).astype(jnp.bfloat16), earlier, preferred_element_type=jnp.float32
@@ -116,7 +130,6 @@
         ).astype(jnp.bfloat16)
 
     place(0)
-    fetch[1].wait()
     values = emb[...].astype(jnp.float32)
     squares = jnp.sum(values * values, axis=1, keepdims=True)
     unit = (values * lax.rsqrt(squares + epsilon)).astype(jnp.bfloat16)
@@ -124,13 +137,24 @@
     buf[OWN, 0:slot, :] = packed[0:slot]
     send[0:part, :] = packed
     pl.semaphore_wait(barrier, groups - 1 + 5)
-    to_prev(0).start()
-    to_next(0).start()
-    for k in range(1, 4):
+    for i in range(CUT):
+        for k in range(1, EARLY + 1):
+            exchange_some(k, i).start()
+        if i == 0:
+            to_prev(0).start()
+            to_next(0).start()
+    for k in range(EARLY + 1, 4):
         exchange(k).start()
     to_partner(0).start()
 
-    for j in range(1, slots // part):
+    def give(j):
+        send[j * part : (j + 1) * part, :] = pack(j)
+        for k in range(4 * j, 4 * j + 4):
+            exchange(k).start()
+
+    place(1)
+    give(1)
+    for j in range(2, slots // part):
         place(j)
     fetch[2].wait()
     rank = rk[...]
@@ -150,10 +174,8 @@
         meta_send[2 * t + 1] = jnp.where(left, turned, tile)
     for k in range(1, groups):
         meta(k).start()
-    for j in range(1, slots // part):
-        send[j * part : (j + 1) * part, :] = pack(j)
-        for k in range(4 * j, 4 * j + 4):
-            exchange(k).start()
+    for j in range(2, slots // part):
+        give(j)
 
     lane_acc[...] = jnp.full(lane_acc.shape, -1.0, jnp.float32)
     sub_acc[...] = jnp.full(sub_acc.shape, -1.0, jnp.float32)
@@ -192,15 +214,25 @@
             return carry
         lax.fori_loop(first, last, step, 0)
 
-    def chunk(i):
-        return pl.multiple_of(i * part, part)
-
-    for k in range(1, groups):
+    half = slots // 2
+
+    def arrived(which, first, last):
+        for k in range(first, last):
+            which(k).wait_recv()
+
+    for i in range(CUT):
+        for k in range(1, EARLY + 1):
+            exchange_some(k, i).wait_recv()
+            to_prev_some(k, i).start()
+            to_next_some(k, i).start()
+    for k in range(1, EARLY + 1):
+        to_partner(k).start()
+    for k in range(EARLY + 1, groups):
         exchange(k).wait_recv()
         to_prev(k).start()
         to_next(k).start()
         to_partner(k).start()
-        if k == 4:
+        if k == 6:
             for i in range(1, groups):
                 meta(i).wait_recv()
             for t in range(tiles):
@@ -209,32 +241,43 @@
             for c in rank_copies:
                 c.start()
             spread(OWN)
-        if k == 10:
+        if k == 7:
+            score(OWN, 0, part, OWN, 0, part)
+        if k == 8:
+            score(OWN, 0, 2 * part, OWN, part, part)
+        if k == 9:
             for c in rank_copies:
                 c.wait_recv()
             spread(PARTNER)
-
-    for j in range(slots // part):
-        score(OWN, 0, (j + 1) * part, OWN, j * part, part)
-    spread(PREV)
-    for k in range(groups):
-        to_partner(k).wait_recv()
-    each(0, 2, lambda i: score(core, 0, slots, 1 - core, pl.multiple_of(core * 2 * part + i * part, part), part))
+        if k == 10:
+            arrived(to_prev, 0, 4)
+            score(OWN, 0, half, NEXT, 0, part)
+        if k == 11:
+            arrived(to_partner, 0, 8)
+            score(PARTNER, 0, half, NEXT, 0, part)
+        if k == 12:
+            spread(PREV)
+        if k == 13:
+            score(OWN, 0, 3 * part, OWN, 2 * part, part)
+        if k == 14:
+            arrived(to_next, 0, 4)
+            score(PREV, 0, part, NEXT, 0, part)
+
+    score(OWN, half, half, NEXT, 0, part)
+    score(OWN, 0, slots, OWN, 3 * part, part)
+    arrived(to_partner, 8, groups)
+    score(PARTNER, half, half, NEXT, 0, part)
+    each(0, 2, lambda i: score(core, 0, slots, 1 - core, pl.multiple_of(core * half + i * part, part), part))
 
     last = slots // part - 1
-    for j in range(last):
+    for j in range(1, last):
         now = j * part
-        for k in range(4 * j, 4 * j + 4):
-            to_prev(k).wait_recv()
+        arrived(to_prev, 4 * j, 4 * j + 4)
         score(OWN, 0, slots, NEXT, now, part)
         score(PARTNER, 0, slots, NEXT, now, part)
-        for k in range(4 * j, 4 * j + 4):
-            to_next(k).wait_recv()
-        if j == 1:
-            each(0, 2, lambda i: score(PREV, 0, 2 * part, NEXT, chunk(i), part))
-        if j >= 2:
-            score(PREV, now, part, NEXT, 0, now)
-            score(PREV, 0, now + part, NEXT, now, part)
+        arrived(to_next, 4 * j, 4 * j + 4)
+        score(PREV, now, part, NEXT, 0, now)
+        score(PREV, 0, now + part, NEXT, now, part)
 
     def gather(which, t):
         tile = jnp.transpose(sub_acc[which, t * 128 : (t + 1) * 128, :])
@@ -256,10 +299,8 @@
             back(which, k).start()
 
     now = last * part
-    for k in range(4 * last, 4 * last + 4):
-        to_next(k).wait_recv()
-    for k in range(4 * last, 4 * last + 4):
-        to_prev(k).wait_recv()
+    arrived(to_next, 4 * last, groups)
+    arrived(to_prev, 4 * last, groups)
     score(PREV, now, part, NEXT, 0, now)
     score(PREV, 0, now + part, NEXT, now, part)
     for t in range(tiles):
@@ -346,7 +387,7 @@
             dma, dma((groups,)),
             dma((4,)), dma((4, groups)),
             dma((4,)), dma((4,)),
-            dma((4,)), dma((4,)),
+            dma((4,)), dma((4,)), dma((EARLY + 1, CUT)),
         ],
         compiler_params=pltpu.CompilerParams(
             collective_id=0, has_side_effects=True, vmem_limit_bytes=48 * 1024 * 1024

time: 70.9 us -> 68.4 us (0.965)
  Pallas kernels: 67.5 us -> 65.1 us
    pallas_call x1, Pallas kernels: 67.5 us -> 65.1 us  [local(): pl.pallas_call(functools.partial(kernel, groups=groups, members=members,...]
where the time goes in v4:
time: 68.4 us; the launch traced here: 68.2 us
  Pallas kernels  65.1 us (95%)
  local copies, waits for them, and re-layouts  3.17 us (5%)
    pallas_call x1, Pallas kernels, local(): pl.pallas_call(functools.partial(kernel, groups=groups, members=members,...  65.1 us
    unnamed x7, local copies, waits for them, and re-layouts  3.17 us

profile of v4, /device:TPU:0, one launch (start us, length us, event | category | flops | bytes accessed | tf_op | source)
XLA Modules:
  0.0 68.2 jit_solution(15465529660872849240)
XLA Ops:
  0.0 0.0 copy-start.1
  0.0 0.7 copy-done.1
  0.7 0.0 copy-start
  0.7 1.2 %copy-done = bf16[512,1024]{1,0:T(8,128)(2,1)S(1)} copy-done((bf16[512,1024]{1,0:T(8,128)(2,1)S(1)}, bf16[512,1024]{1,0:T(8,128)(2,1)}, u32[]{:S(2)}) %copy-start) | copy-done | bytes 1048600
  1.9 0.0 copy-start.2
  1.9 0.7 copy-done.2
  2.6 65.1 %shard_map.37 = f32[1,512]{1,0:T(1,128)S(1)} custom-call(bf16[512,1024]{1,0:T(8,128)(2,1)S(1)} %copy-done, s32[1,512]{1,0:T(1,128)S(1)} %bitcast.4, s32[1,512]{1,0:T(1,128)S(1)} %bitcast.5), custom_call_target="tpu_custom_call" | custom-call | tf_op jit(solution)/shard_map/pallas_call | solution.py:366
  67.7 0.6 copy.5
Async XLA Ops:
  0.0 0.7 copy-start.1
  0.7 1.2 %copy-start = (bf16[512,1024]{1,0:T(8,128)(2,1)S(1)}, bf16[512,1024]{1,0:T(8,128)(2,1)}, u32[]{:S(2)}) copy-start(bf16[512,1024]{1,0:T(8,128)(2,1)} %emb_hbm.1) | copy-start | bytes 3145732
  1.9 0.7 copy-start.2

commit v5 on v4

--- a/solution.py
+++ b/solution.py
@@ -11,6 +11,7 @@
 epsilon = 1e-06
 FAR = 1.0e6
 OWN, PARTNER, NEXT, PREV = range(4)
+SPLIT = 512
 EARLY, CUT = 2, 2
 
 
@@ -191,22 +192,28 @@
             tile = jnp.broadcast_to(rank_lane[which, t : t + 1, :], (128, 128))
             rank_sub[which, t * 128 : (t + 1) * 128, :] = jnp.transpose(tile)
 
-    def score(x, x0, size, y, y0, width):
-        at = pl.ds(x0, size)
-        here = rank_sub[x, at, :]
-        best = jnp.full((size, 128), -1.0, jnp.float32)
-        s = lax.dot_general(
-            buf[x, at, :], buf[y, pl.ds(y0, width), :], (((1,), (1,)), ((), ())),
-            preferred_element_type=jnp.float32,
-        )
+    def score(x, x0, size, y, y0, width, same=False):
+        top = [jnp.full((8, 128), -1.0, jnp.float32)] * (width // 128)
+        for m in range(0, size, SPLIT):
+            cut = min(SPLIT, size - m)
+            at = pl.ds(x0 + m, cut)
+            here = rank_sub[x, at, :]
+            best = sub_acc[x, at, :]
+            s = lax.dot_general(
+                buf[x, at, :], buf[y, pl.ds(y0, width), :], (((1,), (1,)), ((), ())),
+                preferred_element_type=jnp.float32,
+            )
+            for h in range(width // 128):
+                sh = s[:, h * 128 : (h + 1) * 128]
+                there = rank_lane[y, pl.ds(y0 // 128 + h, 1), :]
+                down = there < here
+                best = jnp.maximum(best, jnp.where(down, sh, -1.0))
+                up = jnp.where(here < there, sh, -1.0) if same else jnp.where(down, -1.0, sh)
+                top[h] = jnp.maximum(top[h], jnp.max(up.reshape(cut // 8, 8, 128), axis=0))
+            sub_acc[x, at, :] = best
         for h in range(width // 128):
             t = y0 // 128 + h
-            sh = s[:, h * 128 : (h + 1) * 128]
-            there = rank_lane[y, pl.ds(t, 1), :]
-            best = jnp.maximum(best, jnp.where(there < here, sh, -1.0))
-            up = jnp.where(here < there, sh, -1.0)
-            lane_acc[y, t] = jnp.maximum(lane_acc[y, t], jnp.max(up.reshape(size // 8, 8, 128), axis=0))
-        sub_acc[x, at, :] = jnp.maximum(sub_acc[x, at, :], best)
+            lane_acc[y, t] = jnp.maximum(lane_acc[y, t], top[h])
 
     def each(first, last, body):
         def step(i, carry):
@@ -242,9 +249,9 @@
                 c.start()
             spread(OWN)
         if k == 7:
-            score(OWN, 0, part, OWN, 0, part)
+            score(OWN, 0, part, OWN, 0, part, True)
         if k == 8:
-            score(OWN, 0, 2 * part, OWN, part, part)
+            score(OWN, 0, 2 * part, OWN, part, part, True)
         if k == 9:
             for c in rank_copies:
                 c.wait_recv()
@@ -258,13 +265,13 @@
         if k == 12:
             spread(PREV)
         if k == 13:
-            score(OWN, 0, 3 * part, OWN, 2 * part, part)
+            score(OWN, 0, 3 * part, OWN, 2 * part, part, True)
         if k == 14:
             arrived(to_next, 0, 4)
             score(PREV, 0, part, NEXT, 0, part)
 
     score(OWN, half, half, NEXT, 0, part)
-    score(OWN, 0, slots, OWN, 3 * part, part)
+    score(OWN, 0, slots, OWN, 3 * part, part, True)
     arrived(to_partner, 8, groups)
     score(PARTNER, half, half, NEXT, 0, part)
     each(0, 2, lambda i: score(core, 0, slots, 1 - core, pl.multiple_of(core * half + i * part, part), part))
@@ -295,7 +302,7 @@
         )
 
     def send_back(which):
-        for k in range(1 if which == OWN else 0, groups):
+        for k in reversed(range(1 if which == OWN else 0, groups)):
             back(which, k).start()
 
     now = last * part

time: 68.4 us -> 67.6 us (0.988)
  Pallas kernels: 65.1 us -> 64.3 us
    pallas_call x1, Pallas kernels: 65.1 us -> 64.3 us  [local(): pl.pallas_call(functools.partial(kernel, groups=groups, members=members,...]
where the time goes in v5:
time: 67.6 us; the launch traced here: 67.4 us
  Pallas kernels  64.3 us (95%)
  local copies, waits for them, and re-layouts  3.17 us (5%)
    pallas_call x1, Pallas kernels, local(): pl.pallas_call(functools.partial(kernel, groups=groups, members=members,...  64.3 us
    unnamed x7, local copies, waits for them, and re-layouts  3.17 us

profile of v5, /device:TPU:0, one launch (start us, length us, event | category | flops | bytes accessed | tf_op | source)
XLA Modules:
  0.0 67.4 jit_solution(14422737395478621630)
XLA Ops:
  0.0 0.0 copy-start.1
  0.0 0.7 %copy-done.1 = s32[512]{0:T(512)S(1)} copy-done((s32[512]{0:T(512)S(1)}, s32[512]{0:T(512)}, u32[]{:S(2)}) %copy-start.1) | copy-done | bytes 2072
  0.7 0.0 copy-start
  0.7 1.2 %copy-done = bf16[512,1024]{1,0:T(8,128)(2,1)S(1)} copy-done((bf16[512,1024]{1,0:T(8,128)(2,1)S(1)}, bf16[512,1024]{1,0:T(8,128)(2,1)}, u32[]{:S(2)}) %copy-start) | copy-done | bytes 1048600
  1.9 0.0 copy-start.2
  1.9 0.7 %copy-done.2 = s32[512]{0:T(512)S(1)} copy-done((s32[512]{0:T(512)S(1)}, s32[512]{0:T(512)}, u32[]{:S(2)}) %copy-start.2) | copy-done | bytes 2072
  2.6 64.3 %shard_map.37 = f32[1,512]{1,0:T(1,128)S(1)} custom-call(bf16[512,1024]{1,0:T(8,128)(2,1)S(1)} %copy-done, s32[1,512]{1,0:T(1,128)S(1)} %bitcast.4, s32[1,512]{1,0:T(1,128)S(1)} %bitcast.5), custom_call_target="tpu_custom_call" | custom-call | tf_op jit(solution)/shard_map/pallas_call | solution.py:373
  66.9 0.6 copy.5
Async XLA Ops:
  0.0 0.7 %copy-start.1 = (s32[512]{0:T(512)S(1)}, s32[512]{0:T(512)}, u32[]{:S(2)}) copy-start(s32[512]{0:T(512)} %param.4) | copy-start | bytes 6148
  0.7 1.2 %copy-start = (bf16[512,1024]{1,0:T(8,128)(2,1)S(1)}, bf16[512,1024]{1,0:T(8,128)(2,1)}, u32[]{:S(2)}) copy-start(bf16[512,1024]{1,0:T(8,128)(2,1)} %emb_hbm.1) | copy-start | bytes 3145732
  1.9 0.7 %copy-start.2 = (s32[512]{0:T(512)S(1)}, s32[512]{0:T(512)}, u32[]{:S(2)}) copy-start(s32[512]{0:T(512)} %param.5) | copy-start | bytes 6148

commit v6 on v5

--- a/solution.py
+++ b/solution.py
@@ -25,7 +25,7 @@
     emb_hbm, cl_hbm, rk_hbm, out_ref,
     emb, cl, rk, buf, send, onehot, meta_send, meta_recv, rank_lane, rank_sub, lane_acc, sub_acc,
     result, returned,
-    in_s, meta_s, meta_r, own_s, own_r, rank_s, rank_r, back_s, back_r, early_r,
+    in_s, meta_s, meta_r, own_s, own_r, rank_s, rank_r, back_s, back_r, early_r, wider,
     *, groups, members, slot,
 ):
     rows, depth = emb.shape
@@ -63,10 +63,13 @@
         return {"grp": group_at(k, -1)}
 
     barrier = pltpu.get_barrier_semaphore()
-    for k in range(1, groups):
-        pl.semaphore_signal(barrier, inc=1, device_id=ahead(k), device_id_type=MESH)
-    for peer in (partner, next_same, next_other, prev_same, prev_other):
+    sides = [ahead(k) for k in range(1, 5)]
+    for peer in sides + [partner, next_same, next_other, prev_same, prev_other]:
         pl.semaphore_signal(barrier, inc=1, device_id=peer, device_id_type=MESH)
+
+    def widen(i):
+        for peer in sides:
+            pl.semaphore_signal(wider.at[i], inc=1, device_id=peer, device_id_type=MESH)
 
     def copy(src, dst, ssem, rsem, peer):
         return pltpu.make_async_remote_copy(
@@ -137,7 +140,8 @@
     packed = pack(0)
     buf[OWN, 0:slot, :] = packed[0:slot]
     send[0:part, :] = packed
-    pl.semaphore_wait(barrier, groups - 1 + 5)
+    pl.semaphore_wait(barrier, 9)
+    widen(0)
     for i in range(CUT):
         for k in range(1, EARLY + 1):
             exchange_some(k, i).start()
@@ -150,11 +154,12 @@
 
     def give(j):
         send[j * part : (j + 1) * part, :] = pack(j)
-        for k in range(4 * j, 4 * j + 4):
-            exchange(k).start()
 
     place(1)
     give(1)
+    exchange(4).start()
+    pl.semaphore_wait(wider.at[0], 4)
+    widen(1)
     for j in range(2, slots // part):
         place(j)
     fetch[2].wait()
@@ -173,10 +178,26 @@
         turned = pltpu.roll(tile, slot, 1)
         meta_send[2 * t] = jnp.where(left, tile, turned)
         meta_send[2 * t + 1] = jnp.where(left, turned, tile)
+    pl.semaphore_wait(wider.at[1], 4)
+    widen(2)
+    for k in range(5, 8):
+        exchange(k).start()
+    for i in range(CUT):
+        for k in range(1, EARLY + 1):
+            exchange_some(k, i).wait_recv()
+            to_prev_some(k, i).start()
+            to_next_some(k, i).start()
+    for k in range(1, EARLY + 1):
+        to_partner(k).start()
+    give(2)
+    pl.semaphore_wait(wider.at[2], 4)
     for k in range(1, groups):
         meta(k).start()
-    for j in range(2, slots // part):
-        give(j)
+    for k in range(8, 12):
+        exchange(k).start()
+    give(3)
+    for k in range(12, groups):
+        exchange(k).start()
 
     lane_acc[...] = jnp.full(lane_acc.shape, -1.0, jnp.float32)
     sub_acc[...] = jnp.full(sub_acc.shape, -1.0, jnp.float32)
@@ -227,19 +248,12 @@
         for k in range(first, last):
             which(k).wait_recv()
 
-    for i in range(CUT):
-        for k in range(1, EARLY + 1):
-            exchange_some(k, i).wait_recv()
-            to_prev_some(k, i).start()
-            to_next_some(k, i).start()
-    for k in range(1, EARLY + 1):
-        to_partner(k).start()
     for k in range(EARLY + 1, groups):
         exchange(k).wait_recv()
         to_prev(k).start()
         to_next(k).start()
         to_partner(k).start()
-        if k == 6:
+        if k == 7:
             for i in range(1, groups):
                 meta(i).wait_recv()
             for t in range(tiles):
@@ -248,28 +262,27 @@
             for c in rank_copies:
                 c.start()
             spread(OWN)
-        if k == 7:
+        if k == 8:
             score(OWN, 0, part, OWN, 0, part, True)
-        if k == 8:
+        if k == 9:
             score(OWN, 0, 2 * part, OWN, part, part, True)
-        if k == 9:
+        if k == 11:
             for c in rank_copies:
                 c.wait_recv()
             spread(PARTNER)
-        if k == 10:
+        if k == 12:
             arrived(to_prev, 0, 4)
             score(OWN, 0, half, NEXT, 0, part)
-        if k == 11:
+        if k == 13:
             arrived(to_partner, 0, 8)
             score(PARTNER, 0, half, NEXT, 0, part)
+        if k == 14:
+            spread(PREV)
         if k == 12:
-            spread(PREV)
-        if k == 13:
             score(OWN, 0, 3 * part, OWN, 2 * part, part, True)
-        if k == 14:
-            arrived(to_next, 0, 4)
-            score(PREV, 0, part, NEXT, 0, part)
-
+
+    arrived(to_next, 0, 4)
+    score(PREV, 0, part, NEXT, 0, part)
     score(OWN, half, half, NEXT, 0, part)
     score(OWN, 0, slots, OWN, 3 * part, part, True)
     arrived(to_partner, 8, groups)
@@ -395,6 +408,7 @@
             dma((4,)), dma((4, groups)),
             dma((4,)), dma((4,)),
             dma((4,)), dma((4,)), dma((EARLY + 1, CUT)),
+            pltpu.SemaphoreType.REGULAR((3,)),
         ],
         compiler_params=pltpu.CompilerParams(
             collective_id=0, has_side_effects=True, vmem_limit_bytes=48 * 1024 * 1024

time: 67.6 us -> 67.6 us (level)
  no operation moved by 1% of the time
where the time goes in v6:
time: 67.6 us; the launch traced here: 67.4 us
  Pallas kernels  64.2 us (95%)
  local copies, waits for them, and re-layouts  3.17 us (5%)
    pallas_call x1, Pallas kernels, local(): pl.pallas_call(functools.partial(kernel, groups=groups, members=members,...  64.2 us
    unnamed x7, local copies, waits for them, and re-layouts  3.17 us

profile of v6, /device:TPU:0, one launch (start us, length us, event | category | flops | bytes accessed | tf_op | source)
XLA Modules:
  0.0 67.4 jit_solution(15587259093664156903)
XLA Ops:
  0.0 0.0 copy-start.1
  0.0 0.7 %copy-done.1 = s32[512]{0:T(512)S(1)} copy-done((s32[512]{0:T(512)S(1)}, s32[512]{0:T(512)}, u32[]{:S(2)}) %copy-start.1) | copy-done | bytes 2072
  0.7 0.0 copy-start
  0.7 1.2 %copy-done = bf16[512,1024]{1,0:T(8,128)(2,1)S(1)} copy-done((bf16[512,1024]{1,0:T(8,128)(2,1)S(1)}, bf16[512,1024]{1,0:T(8,128)(2,1)}, u32[]{:S(2)}) %copy-start) | copy-done | bytes 1048600
  1.9 0.0 copy-start.2
  1.9 0.7 %copy-done.2 = s32[512]{0:T(512)S(1)} copy-done((s32[512]{0:T(512)S(1)}, s32[512]{0:T(512)}, u32[]{:S(2)}) %copy-start.2) | copy-done | bytes 2072
  2.6 64.2 %shard_map.37 = f32[1,512]{1,0:T(1,128)S(1)} custom-call(bf16[512,1024]{1,0:T(8,128)(2,1)S(1)} %copy-done, s32[1,512]{1,0:T(1,128)S(1)} %bitcast.4, s32[1,512]{1,0:T(1,128)S(1)} %bitcast.5), custom_call_target="tpu_custom_call" | custom-call | tf_op jit(solution)/shard_map/pallas_call | solution.py:386
  66.8 0.6 copy.5
Async XLA Ops:
  0.0 0.7 %copy-start.1 = (s32[512]{0:T(512)S(1)}, s32[512]{0:T(512)}, u32[]{:S(2)}) copy-start(s32[512]{0:T(512)} %param.4) | copy-start | bytes 6148
  0.7 1.2 %copy-start = (bf16[512,1024]{1,0:T(8,128)(2,1)S(1)}, bf16[512,1024]{1,0:T(8,128)(2,1)}, u32[]{:S(2)}) copy-start(bf16[512,1024]{1,0:T(8,128)(2,1)} %emb_hbm.1) | copy-start | bytes 3145732
  1.9 0.7 %copy-start.2 = (s32[512]{0:T(512)S(1)}, s32[512]{0:T(512)}, u32[]{:S(2)}) copy-start(s32[512]{0:T(512)} %param.5) | copy-start | bytes 6148

commit v7 on v5

--- a/solution.py
+++ b/solution.py
@@ -316,12 +316,15 @@
     send_back(PREV)
     for t in range(tiles):
         result[PARTNER, t] = jnp.maximum(gather(PARTNER, t), along(PARTNER, t))
-    score(OWN, 0, slots, NEXT, now, part)
+    score(OWN, 0, half, NEXT, now, part)
+    for t in range(tiles // 2):
+        result[OWN, t] = jnp.maximum(gather(OWN, t), along(OWN, t))
+    score(OWN, half, half, NEXT, now, part)
     for t in range(tiles):
         result[NEXT, t] = along(NEXT, t)
     send_back(NEXT)
     send_back(PARTNER)
-    for t in range(tiles):
+    for t in range(tiles // 2, tiles):
         result[OWN, t] = jnp.maximum(gather(OWN, t), along(OWN, t))
     send_back(OWN)
 

time: 67.6 us -> 67.7 us (level)
  no operation moved by 1% of the time
where the time goes in v7:
time: 67.7 us; the launch traced here: 67.5 us
  Pallas kernels  64.3 us (95%)
  local copies, waits for them, and re-layouts  3.17 us (5%)
    pallas_call x1, Pallas kernels, local(): pl.pallas_call(functools.partial(kernel, groups=groups, members=members,...  64.3 us
    unnamed x7, local copies, waits for them, and re-layouts  3.17 us

profile of v7, /device:TPU:0, one launch (start us, length us, event | category | flops | bytes accessed | tf_op | source)
XLA Modules:
  0.0 67.5 jit_solution(16767295584249251394)
XLA Ops:
  0.0 0.0 copy-start.1
  0.0 0.7 %copy-done.1 = s32[512]{0:T(512)S(1)} copy-done((s32[512]{0:T(512)S(1)}, s32[512]{0:T(512)}, u32[]{:S(2)}) %copy-start.1) | copy-done | bytes 2072
  0.7 0.0 copy-start
  0.7 1.2 %copy-done = bf16[512,1024]{1,0:T(8,128)(2,1)S(1)} copy-done((bf16[512,1024]{1,0:T(8,128)(2,1)S(1)}, bf16[512,1024]{1,0:T(8,128)(2,1)}, u32[]{:S(2)}) %copy-start) | copy-done | bytes 1048600
  1.9 0.0 copy-start.2
  1.9 0.7 %copy-done.2 = s32[512]{0:T(512)S(1)} copy-done((s32[512]{0:T(512)S(1)}, s32[512]{0:T(512)}, u32[]{:S(2)}) %copy-start.2) | copy-done | bytes 2072
  2.6 64.3 %shard_map.37 = f32[1,512]{1,0:T(1,128)S(1)} custom-call(bf16[512,1024]{1,0:T(8,128)(2,1)S(1)} %copy-done, s32[1,512]{1,0:T(1,128)S(1)} %bitcast.4, s32[1,512]{1,0:T(1,128)S(1)} %bitcast.5), custom_call_target="tpu_custom_call" | custom-call | tf_op jit(solution)/shard_map/pallas_call | solution.py:376
  66.9 0.6 copy.5
Async XLA Ops:
  0.0 0.7 %copy-start.1 = (s32[512]{0:T(512)S(1)}, s32[512]{0:T(512)}, u32[]{:S(2)}) copy-start(s32[512]{0:T(512)} %param.4) | copy-start | bytes 6148
  0.7 1.2 %copy-start = (bf16[512,1024]{1,0:T(8,128)(2,1)S(1)}, bf16[512,1024]{1,0:T(8,128)(2,1)}, u32[]{:S(2)}) copy-start(bf16[512,1024]{1,0:T(8,128)(2,1)} %emb_hbm.1) | copy-start | bytes 3145732
  1.9 0.7 %copy-start.2 = (s32[512]{0:T(512)S(1)}, s32[512]{0:T(512)}, u32[]{:S(2)}) copy-start(s32[512]{0:T(512)} %param.5) | copy-start | bytes 6148
